TPU v7x, 8 devices: a whole 2x2x1 slice. The times are simulated.
8 devices in a mesh: dp: 1 (over z), tp: 2 (over y), sp: 4 (over x, core).
Axes of the slice: x: 2, y: 2, z: 1, core: 2. Of those that a mesh axis runs over, the one named last changes fastest.
Arguments:
- hidden: bfloat16 [32, 5120], P('dp')
- norm_gain: float32 [5120], replicated
- w_query: bfloat16 [5120, 5120], P(None, 'tp')
- w_key: bfloat16 [5120, 5120], P(None, 'tp')
- w_value: bfloat16 [5120, 5120], P(None, 'tp')
- w_out: bfloat16 [5120, 5120], P('tp')
- k_cache: bfloat16 [32, 1024, 40, 128], P('dp', 'sp', 'tp')
- v_cache: bfloat16 [32, 1024, 40, 128], P('dp', 'sp', 'tp')
- positions: int32 [32], P('dp')
Outputs:
- output 1: bfloat16 [32, 5120], P('dp')
- output 2: bfloat16 [32, 1024, 40, 128], P('dp', 'sp', 'tp')
- output 3: bfloat16 [32, 1024, 40, 128], P('dp', 'sp', 'tp')
All inputs are finite; a program needn't handle non-finite values.
Results may differ from a plain program's by a relative error of at most 0.00274627.
Values sent between devices are 32-bit elements.
A program may use at most 1.25 GiB of HBM per device.

v0:
```python
import jax
import jax.numpy as jnp
from jax import lax
from jax.sharding import PartitionSpec as P

ROPE_BASE = 1000000.0
EPS = 1e-5
NEG_BIG = -1e30


def rotary(tensor, positions):
    half_dim = tensor.shape[-1] // 2
    inv_freq = 1.0 / (ROPE_BASE ** (jnp.arange(half_dim, dtype=jnp.float32) * 2.0 / tensor.shape[-1]))
    angles = positions.astype(jnp.float32)[:, None, None] * inv_freq[None, None, :]
    cosine = jnp.cos(angles)
    sine_val = jnp.sin(angles)
    first_half = tensor[..., :half_dim]
    second_half = tensor[..., half_dim:]
    return jnp.concatenate([first_half * cosine - second_half * sine_val, first_half * sine_val + second_half * cosine], axis=-1)


def solution(mesh):
    def local_step(hidden, norm_gain, w_query, w_key, w_value, w_out, k_cache, v_cache, positions):
        batch_size, seq_local, kv_local, head_dim = k_cache.shape
        q_local = w_query.shape[1] // head_dim
        group_size = q_local // kv_local
        resid_f32 = hidden.astype(jnp.float32)
        normed = (resid_f32 * lax.rsqrt(jnp.mean(resid_f32 * resid_f32, axis=-1, keepdims=True) + EPS) * norm_gain).astype(jnp.bfloat16)
        q_proj = jnp.dot(normed, w_query, preferred_element_type=jnp.float32).reshape(batch_size, q_local, head_dim)
        k_proj = jnp.dot(normed, w_key, preferred_element_type=jnp.float32).reshape(batch_size, kv_local, head_dim)
        v_new = jnp.dot(normed, w_value, preferred_element_type=jnp.float32).astype(jnp.bfloat16).reshape(batch_size, kv_local, head_dim)
        q_rot = rotary(q_proj, positions).astype(jnp.bfloat16).reshape(batch_size, kv_local, group_size, head_dim)
        k_new = rotary(k_proj, positions).astype(jnp.bfloat16)
        slot_pos = lax.axis_index("sp") * seq_local + jnp.arange(seq_local)
        slot_mask = (slot_pos[None, :] == positions[:, None])[:, :, None, None]
        k_updated = jnp.where(slot_mask, k_new[:, None], k_cache)
        v_updated = jnp.where(slot_mask, v_new[:, None], v_cache)
        scores = jnp.einsum("bkgd,bskd->bkgs", q_rot, k_updated, preferred_element_type=jnp.float32) * (head_dim ** -0.5)
        valid_mask = (slot_pos[None, :] <= positions[:, None])[:, None, None, :]
        scores = jnp.where(valid_mask, scores, NEG_BIG)
        local_max = jnp.max(scores, axis=-1, keepdims=True)
        exp_weights = jnp.where(valid_mask, jnp.exp(scores - local_max), 0.0)
        local_sum = jnp.sum(exp_weights, axis=-1, keepdims=True)
        local_acc = jnp.einsum("bkgs,bskd->bkgd", exp_weights.astype(jnp.bfloat16), v_updated, preferred_element_type=jnp.float32)
        block_stats = jnp.concatenate([local_acc, local_sum, local_max], axis=-1)
        gathered = lax.all_gather(block_stats, "sp")
        all_max = gathered[..., head_dim + 1:]
        global_max = jnp.max(all_max, axis=0)
        rescale = jnp.exp(all_max - global_max)
        total_sum = jnp.sum(gathered[..., head_dim:head_dim + 1] * rescale, axis=0)
        total_acc = jnp.sum(gathered[..., :head_dim] * rescale, axis=0)
        attn_out = (total_acc / total_sum).astype(jnp.bfloat16).reshape(batch_size, q_local * head_dim)
        part_proj = jnp.dot(attn_out, w_out, preferred_element_type=jnp.float32)
        proj_out = lax.psum(part_proj, "tp")
        return (resid_f32 + proj_out).astype(jnp.bfloat16), k_updated, v_updated

    cache_spec = P("dp", "sp", "tp", None)
    specs_in = (P("dp", None), P(None), P(None, "tp"), P(None, "tp"), P(None, "tp"), P("tp", None), cache_spec, cache_spec, P("dp"))
    specs_out = (P("dp", None), cache_spec, cache_spec)
    return jax.shard_map(local_step, mesh=mesh, in_specs=specs_in, out_specs=specs_out, check_vma=False)
```

profile of v0, /device:TPU:0, one launch (start us, length us, event | category | flops | bytes accessed | tf_op | source)
XLA Modules:
  0.0 214.0 jit_solution(2406355514687781774)
XLA Ops:
  7.3 0.7 convert_element_type.36
  7.9 1.1 fusion.3
  9.1 0.7 broadcast_compare_fusion.1
  9.9 13.3 %convolution_convert_fusion = bf16[32,2560]{1,0:T(8,128)(2,1)S(1)} fusion(bf16[5120,2560]{1,0:T(8,128)(2,1)} %param.13, bf16[32,5120]{1,0:T(8,128)(2,1)} %param.9, f32[5120]{0:T(1024)} %param.10, f32[32]{0:T(128)S(1)} %add_rsqrt_fusion), kind=kOutput, calls=%fused_computation.2 | convolution fusion | flops 839598080 | bytes 26726528 | tf_op jit(solution)/shard_map/dot_general | solution.py:31
  23.3 11.1 %fusion.20 = f32[32,2560]{1,0:T(8,128)S(1)} fusion(bf16[5120,2560]{1,0:T(8,128)(2,1)} %param.12, bf16[32,5120]{1,0:T(8,128)(2,1)S(1)} %copy-done, f32[5120]{0:T(1024)S(1)} %copy-done.1, f32[32]{0:T(128)S(1)} %add_rsqrt_fusion), kind=kOutput, calls=%fused_computation.45 | convolution fusion | flops 839516160 | bytes 26890368 | tf_op jit(solution)/shard_map/dot_general | solution.py:30
  34.4 10.9 %fusion.22 = f32[32,2560]{1,0:T(8,128)S(1)} fusion(bf16[5120,2560]{1,0:T(8,128)(2,1)} %param.11, bf16[32,5120]{1,0:T(8,128)(2,1)S(1)} %copy-done, f32[5120]{0:T(1024)S(1)} %copy-done.1, f32[32]{0:T(128)S(1)} %add_rsqrt_fusion), kind=kOutput, calls=%fused_computation.46 | convolution fusion | flops 839516160 | bytes 26890368 | tf_op jit(solution)/shard_map/dot_general | solution.py:29
  45.3 0.1 multiply_cosine_fusion
  45.5 0.3 subtract_convert_fusion.1
  46.1 55.0 %broadcast_select_fusion = (bf16[32,256,20,128]{3,1,2,0:T(8,128)(2,1)}, bf16[32,256,20,128]{3,1,2,0:T(8,128)(2,1)}) fusion(bf16[32,256,20,128]{3,1,2,0:T(8,128)(2,1)} %param.16, pred[32,256]{1,0:T(8,128)(4,1)S(1)} %get-tuple-element.16, bf16[32,20,128]{2,1,0:T(8,128)(2,1)S(1)} %broadcast_in_dim.69, bf16[32,256,20,128]{3,1,2,0:T(8,128)(2,1)} %param.15, ...), kind=kLoop, calls=%fused_computation | loop fusion | flops 41943040 | bytes 168108032 | tf_op jit(solution)/shard_map/jit(_where)/select_n | solution.py:37
  101.0 16.8 %fusion.15 = f32[32,20,1,256]{3,2,1,0:T(1,128)S(1)} fusion(bf16[32,256,20,128]{3,1,2,0:T(8,128)(2,1)} %get-tuple-element.14, bf16[32,20,128,1]{2,1,0,3:T(8,128)(2,1)S(1)} %maximum_bitcast_fusion), kind=kOutput, calls=%fused_computation.33 | convolution fusion | flops 41943040 | bytes 42762240 | tf_op jit(solution)/shard_map/bkgd,bskd->bkgs/dot_general | solution.py:38
  117.8 0.3 fusion.12
  118.1 0.3 fusion.13
  118.4 15.8 %fusion.8 = f32[32,20,1,128]{3,2,1,0:T(1,128)S(1)} fusion(bf16[32,256,20,128]{3,1,2,0:T(8,128)(2,1)} %get-tuple-element.13, bf16[32,20,256,1]{2,0,1,3:T(8,128)(2,1)S(1)} %get-tuple-element.5), kind=kOutput, calls=%fused_computation.20 | convolution fusion | flops 41943040 | bytes 42598400 | tf_op jit(solution)/shard_map/bkgs,bskd->bkgd/dot_general | solution.py:44
  134.2 0.2 copy.25
  134.5 0.2 copy.24
  134.7 1.0 pad_maximum_fusion
  135.7 25.4 %all-gather.3.cloned.1.call-done = f32[128,20,1,130]{3,0,1,2:T(8,128)} async-done(((f32[32,20,1,130]{3,0,1,2:T(8,128)}), f32[128,20,1,130]{3,0,1,2:T(8,128)}) %all-gather.3.cloned.1.call-update) | async-done | bytes 1331216 | tf_op jit(solution)/shard_map/all_gather | solution.py:46
  161.1 1.9 slice_reduce_fusion
  163.0 2.7 %fusion.2 = (f32[4,32,20]{1,0,2:T(4,128)S(1)}, f32[32,20]{0,1:T(8,128)S(1)}) fusion(f32[4,32,20,1,130]{4,1,0,2,3:T(8,128)} %bitcast.42, f32[32,20]{0,1:T(8,128)S(1)} %slice_reduce_fusion), kind=kLoop, calls=%fused_computation.9 | loop fusion | flops 7040 | bytes 35840 | tf_op jit(solution)/shard_map/exp | solution.py:49
  165.7 1.8 fusion.1
  167.5 0.2 div.31
  167.7 11.7 %fusion.17 = f32[32,5120]{1,0:T(8,128)} fusion(bf16[2560,5120]{1,0:T(8,128)(2,1)} %param.14, f32[4,8,20,128]{3,2,1,0:T(8,128)S(1)} %bitcast.44, f32[32,20,128]{2,0,1:T(8,128)S(1)} %fusion.1), kind=kOutput, calls=%fused_computation.37 | convolution fusion | flops 839024640 | bytes 27525120 | tf_op jit(solution)/shard_map/dot_general | solution.py:53
  179.4 25.9 %all-reduce.2.cloned.1.call-done = f32[32,5120]{1,0:T(8,128)} async-done(((f32[32,5120]{1,0:T(8,128)}), f32[32,5120]{1,0:T(8,128)}) %all-reduce.2.cloned.1.call-update) | async-done | bytes 655376 | tf_op jit(solution)/shard_map/psum | solution.py:54
  205.3 1.9 fusion.6
  (18 shorter events, 0.7 us)
Async XLA Ops:
  7.2 16.1 %copy-start = (bf16[32,5120]{1,0:T(8,128)(2,1)S(1)}, bf16[32,5120]{1,0:T(8,128)(2,1)}, u32[]{:S(2)}) copy-start(bf16[32,5120]{1,0:T(8,128)(2,1)} %param.9) | copy-start | bytes 983044
  7.2 16.1 %copy-start.1 = (f32[5120]{0:T(1024)S(1)}, f32[5120]{0:T(1024)}, u32[]{:S(2)}) copy-start(f32[5120]{0:T(1024)} %param.10) | copy-start | bytes 61444
  7.2 153.9 %all-gather.3.cloned.1.call-start = ((), (), s32[]{:S(2)}) async-start(), calls=%async_computation.1 | async-start | bytes 3276800 | tf_op jit(solution)/shard_map/all_gather | solution.py:46
  135.7 69.6 %all-reduce.2.cloned.1.call-start = ((), (), s32[]{:S(2)}) async-start(), calls=%async_computation | async-start | bytes 1310720 | tf_op jit(solution)/shard_map/psum | solution.py:54
Sparse Core Ops, SparseCore 0:
  135.8 25.2 all-gather.2
  179.5 25.6 all-reduce.1
where the time goes:
time: 214 us
  matrix products  79.5 us (37%)
  other arithmetic  68.1 us (32%)
  waiting for transfers between devices  51.2 us (24%)
  between operations  14.2 us (7%)
    select_n x1, other arithmetic, local_step(): v_updated = jnp.where(slot_mask, v_new[:, None], v_cache)  55 us
    psum x1, waiting for transfers between devices, local_step(): proj_out = lax.psum(part_proj, 'tp')  25.9 us
    all_gather x1, waiting for transfers between devices, local_step(): gathered = lax.all_gather(block_stats, 'sp')  25.4 us
    dot_general x1, matrix products, local_step(): jnp.einsum('bkgd,bskd->bkgs', q_rot, k_updated, preferred_element_type=jn...  16.8 us
    dot_general x1, matrix products, local_step(): jnp.einsum('bkgs,bskd->bkgd', exp_weights.astype(jnp.bfloat16), v_updated...  15.8 us
    dot_general x1, matrix products, local_step(): jnp.dot(normed, w_value, preferred_element_type=jnp.float32)  13.3 us
    dot_general x1, matrix products, local_step(): part_proj = jnp.dot(attn_out, w_out, preferred_element_type=jnp.float32)  11.7 us
    dot_general x1, matrix products, local_step(): jnp.dot(normed, w_key, preferred_element_type=jnp.float32)  11.1 us
  transfers between devices with their start and end apart: 2, of which 2 were waited for; matrix products, arithmetic and copies ran while one was open for 0% of the time, Pallas kernels for 0%

commit v1 on v0

v1 whole, which is shorter than its diff:
```python
import jax
import jax.numpy as jnp
import numpy as np
from jax import lax
from jax.experimental import pallas as pl
from jax.experimental.pallas import tpu as pltpu
from jax.sharding import PartitionSpec as P

ROPE_BASE = 1000000.0
EPS = 1e-5
NEG_BIG = -1e30
MESH = pl.DeviceIdType.MESH
ANY = pl.BlockSpec(memory_space=pl.ANY)
VMEM = pl.BlockSpec(memory_space=pltpu.VMEM)
SMEM = pl.BlockSpec(memory_space=pltpu.SMEM)

B = 32
D = 5120
HL = 20
HD = 128
SL = 256
HS = 5
CW = HS * HD
KC = 512
NKC = D // KC
OC = 1280
OCH = 256
NOC = OC // OCH
SLOTS = 12
AHEAD = 8


def peers():
    sp = lax.axis_index("sp")
    across = lax.rem(sp + 2, 4)
    core = sp + 1 - 2 * lax.rem(sp, 2)
    return sp, across, core


def remote(src, dst, send, recv, dev):
    return pltpu.make_async_remote_copy(src_ref=src, dst_ref=dst, send_sem=send, recv_sem=recv,
                                        device_id=dev, device_id_type=MESH)


def qkv_kernel(pos_ref, h_ref, gain_ref, freq_ref, wq_ref, wk_ref, wv_ref, out_ref,
               wbuf, xn, g, wsem, ssem, rsem):
    sp, across, core = peers()
    bar = pltpu.get_barrier_semaphore()
    for dev in (across, core):
        pl.semaphore_signal(bar, inc=1, device_id={"sp": dev}, device_id_type=MESH)
    cols = pl.ds(pl.multiple_of(sp * CW, HD), CW)

    def chunk_copy(kind, c):
        src = (wq_ref, wk_ref, wv_ref)[kind]
        rows = pl.ds(pl.multiple_of(c * KC, KC), KC)
        return pltpu.make_async_copy(src.at[rows, cols], wbuf.at[kind, rows], wsem.at[kind, c])

    for kind in range(3):
        for c in range(NKC):
            chunk_copy(kind, c).start()

    x = h_ref[...].astype(jnp.float32)
    inv = lax.rsqrt(jnp.mean(x * x, axis=-1, keepdims=True) + EPS)
    xn[...] = (x * inv * gain_ref[...]).astype(jnp.bfloat16)
    row = lax.broadcasted_iota(jnp.int32, (B, HD), 0)
    lane = lax.broadcasted_iota(jnp.int32, (B, HD), 1)
    pos = jnp.zeros((B, HD), jnp.int32)
    for b in range(B):
        pos = jnp.where(row == b, pos_ref[b], pos)
    angles = pos.astype(jnp.float32) * freq_ref[...]
    cosine = jnp.cos(angles)
    sine = jnp.sin(angles)
    sine = jnp.where(lane < HD // 2, -sine, sine)
    pl.semaphore_wait(bar, 2)

    own = pl.ds(pl.multiple_of(sp * HS * B, B), HS * B)
    far = pl.ds(pl.multiple_of(across * HS * B, B), HS * B)

    def copies(kind):
        return (remote(g.at[kind, own], g.at[kind, own], ssem.at[kind, 0], rsem.at[kind, 0], {"sp": across}),
                remote(g.at[kind, own], g.at[kind, own], ssem.at[kind, 1], rsem.at[kind, 1], {"sp": core}),
                remote(g.at[kind, far], g.at[kind, far], ssem.at[kind, 2], rsem.at[kind, 2], {"sp": core}))

    for kind in range(3):
        def body(c, acc):
            chunk_copy(kind, c).wait()
            rows = pl.ds(pl.multiple_of(c * KC, KC), KC)
            return acc + jnp.dot(xn[:, rows], wbuf[kind, rows, :], preferred_element_type=jnp.float32)
        acc = lax.fori_loop(0, NKC, body, jnp.zeros((B, CW), jnp.float32))
        for i in range(HS):
            u = acc[:, i * HD:(i + 1) * HD]
            if kind < 2:
                u = u * cosine + pltpu.roll(u, HD // 2, 1) * sine
            g[kind, pl.ds(pl.multiple_of(sp * HS * B + i * B, B), B), :] = u.astype(jnp.bfloat16).astype(jnp.float32)
        first, second, _ = copies(kind)
        first.start()
        second.start()
        if kind > 0:
            prev = copies(kind - 1)
            prev[0].wait_recv()
            prev[2].start()
    last = copies(2)
    last[0].wait_recv()
    last[2].start()
    for kind in range(3):
        for i, c in enumerate(copies(kind)):
            if i == 0:
                c.wait_send()
            else:
                c.wait()
    out_ref[...] = g[...]


def cache_kernel(pos_ref, g_ref, k_ref, v_ref, ko_ref, vo_ref, acc_ref, ml_ref,
                 kbuf, vbuf, sbuf, rsem, wsem):
    base = lax.axis_index("sp") * SL

    def reads(b):
        slot = lax.rem(b, SLOTS)
        return (pltpu.make_async_copy(k_ref.at[b], kbuf.at[slot], rsem.at[0, slot]),
                pltpu.make_async_copy(v_ref.at[b], vbuf.at[slot], rsem.at[1, slot]))

    def writes(b):
        slot = lax.rem(b, SLOTS)
        return (pltpu.make_async_copy(kbuf.at[slot], ko_ref.at[b], wsem.at[0, slot]),
                pltpu.make_async_copy(vbuf.at[slot], vo_ref.at[b], wsem.at[1, slot]))

    for b in range(AHEAD):
        for c in reads(b):
            c.start()
    ml_ref[...] = jnp.zeros_like(ml_ref)

    def arrive(b):
        slot = lax.rem(b, SLOTS)
        for c in reads(b):
            c.wait()
        at = pos_ref[b] - base

        @pl.when((at >= 0) & (at < SL))
        def _():
            start = pl.multiple_of((at // 16) * 16, 16)
            hit = lax.broadcasted_iota(jnp.int32, (16, HD), 0) == at - start
            for kind, buf in ((1, kbuf), (2, vbuf)):
                for h in range(HL):
                    new = jnp.broadcast_to(g_ref[kind, pl.ds(h * B + b, 1), :], (16, HD))
                    old = buf[slot, h, pl.ds(start, 16), :].astype(jnp.float32)
                    buf[slot, h, pl.ds(start, 16), :] = jnp.where(hit, new, old).astype(jnp.bfloat16)

    qrow = lax.broadcasted_iota(jnp.int32, (HL, HD), 0)
    prow = lax.broadcasted_iota(jnp.int32, (HL, SL), 0)
    pcol = lax.broadcasted_iota(jnp.int32, (HL, SL), 1)
    mlane = lax.broadcasted_iota(jnp.int32, (HL, HD), 1)

    def score(b):
        slot = lax.rem(b, SLOTS)
        q = g_ref[0, pl.ds(b, HL, stride=B), :]
        s = jnp.zeros((HL, SL), jnp.float32)
        for h in range(HL):
            qh = jnp.where(qrow == h, q, 0.0).astype(jnp.bfloat16)
            s = s + lax.dot_general(qh, kbuf[slot, h], (((1,), (1,)), ((), ())), preferred_element_type=jnp.float32)
        sbuf[lax.rem(b, 2)] = s * (HD ** -0.5)

    def value(b):
        slot = lax.rem(b, SLOTS)
        valid = pcol <= pos_ref[b] - base
        s = jnp.where(valid, sbuf[lax.rem(b, 2)], NEG_BIG)
        m = jnp.max(s, axis=-1, keepdims=True)
        p = jnp.where(valid, jnp.exp(s - m), 0.0)
        total = jnp.sum(p, axis=-1, keepdims=True)
        o = jnp.zeros((HL, HD), jnp.float32)
        for h in range(HL):
            ph = jnp.where(prow == h, p, 0.0).astype(jnp.bfloat16)
            o = o + jnp.dot(ph, vbuf[slot, h], preferred_element_type=jnp.float32)
        acc_ref[pl.ds(b, HL, stride=B), :] = o
        ml_ref[...] = jnp.where(mlane == b, m, jnp.where(mlane == b + B, total, ml_ref[...]))

    def ahead(b):
        @pl.when(b + AHEAD < B)
        def _():
            @pl.when(b + AHEAD >= SLOTS)
            def _():
                for c in writes(b + AHEAD - SLOTS):
                    c.wait()
            for c in reads(b + AHEAD):
                c.start()

    arrive(0)
    ahead(0)
    score(0)
    writes(0)[0].start()

    @pl.loop(1, B)
    def _(b):
        arrive(b)
        ahead(b)
        score(b)
        value(b - 1)
        writes(b)[0].start()
        writes(b - 1)[1].start()

    value(B - 1)
    writes(B - 1)[1].start()
    for b in range(B - SLOTS, B):
        for c in writes(b):
            c.wait()


def out_kernel(acc_ref, ml_ref, h_ref, w_ref, out_ref,
               wbuf, mlbuf, send1, r1, pair, r2, oall, ypart, yin, yall,
               wsem, mlsend, mlrecv, ssem, rsem, ysend, yrecv):
    sp, across, core = peers()
    diag = 3 - sp
    tp = lax.axis_index("tp")
    c01 = lax.rem(sp, 2)
    bar = pltpu.get_barrier_semaphore()
    half = HL // 2
    hr = half * B

    wcopies = [pltpu.make_async_copy(w_ref.at[pl.ds(i * KC, KC), pl.ds(pl.multiple_of(sp * OC, HD), OC)],
                                     wbuf.at[pl.ds(i * KC, KC)], wsem.at[i]) for i in range(HL * HD // KC)]
    for c in wcopies:
        c.start()
    for dev in (across, core, diag):
        pl.semaphore_signal(bar, inc=1, device_id={"sp": dev}, device_id_type=MESH)
    pl.semaphore_signal(bar, inc=1, device_id={"tp": 1 - tp}, device_id_type=MESH)
    mlbuf[0] = ml_ref[...]
    send1[...] = acc_ref[pl.ds(pl.multiple_of((1 - c01) * hr, B), hr), :]
    pl.semaphore_wait(bar, 4)

    mlc = [remote(mlbuf.at[0], mlbuf.at[i + 1], mlsend.at[i], mlrecv.at[i], {"sp": dev})
           for i, dev in enumerate((core, across, diag))]
    c1 = remote(send1, r1, ssem.at[0], rsem.at[0], {"sp": core})
    mlc[0].start()
    c1.start()
    mlc[1].start()
    mlc[2].start()

    def columns(table):
        t = jnp.where(c01 == 0, table[:half], table[half:])
        t = jnp.concatenate([t, jnp.zeros((HD - half, HD), jnp.float32)], axis=0)
        return jnp.transpose(t)

    mlc[0].wait_recv()
    own = mlbuf[0]
    other = mlbuf[1]
    m_pair = jnp.maximum(own, other)
    f_own = columns(jnp.exp(own - m_pair))
    f_other = columns(jnp.exp(other - m_pair))
    c1.wait_recv()
    for i in range(half):
        mine = acc_ref[pl.ds(pl.multiple_of(c01 * hr + i * B, B), B), :]
        theirs = r1[i * B:(i + 1) * B, :]
        pair[i * B:(i + 1) * B, :] = mine * f_own[:B, i:i + 1] + theirs * f_other[:B, i:i + 1]
    c2 = remote(pair, r2, ssem.at[1], rsem.at[1], {"sp": across})
    c2.start()

    mlc[1].wait_recv()
    mlc[2].wait_recv()
    tabs = [mlbuf[i] for i in range(4)]
    m_far = jnp.maximum(tabs[2], tabs[3])
    m_all = jnp.maximum(m_pair, m_far)
    total = jnp.zeros((HL, HD), jnp.float32)
    for t in tabs:
        total = total + jnp.exp(t - m_all) * pltpu.roll(t, HD - B, 1)
    lane = lax.broadcasted_iota(jnp.int32, (HL, HD), 1)
    total = jnp.where(lane < B, total, 1.0)
    g_pair = columns(jnp.exp(m_pair - m_all) / total)
    g_far = columns(jnp.exp(m_far - m_all) / total)
    c2.wait_recv()
    for i in range(half):
        o = pair[i * B:(i + 1) * B, :] * g_pair[:B, i:i + 1] + r2[i * B:(i + 1) * B, :] * g_far[:B, i:i + 1]
        oall[pl.ds(pl.multiple_of(c01 * hr + i * B, B), B), :] = o
    mine = pl.ds(pl.multiple_of(c01 * hr, B), hr)
    c3 = remote(oall.at[mine], oall.at[mine], ssem.at[2], rsem.at[2], {"sp": core})
    c3.start()
    for c in wcopies:
        c.wait()
    c3.wait_recv()

    lhs = [jnp.concatenate([oall[(2 * i) * B:(2 * i + 1) * B, :], oall[(2 * i + 1) * B:(2 * i + 2) * B, :]],
                           axis=1).astype(jnp.bfloat16) for i in range(half)]

    def piece(j):
        return (remote(ypart.at[j], yin.at[j], ysend.at[0, j], yrecv.at[0, j], {"tp": 1 - tp}),
                remote(yall.at[sp, j], yall.at[sp, j], ysend.at[1, j], yrecv.at[1, j], {"sp": across}),
                remote(yall.at[sp, j], yall.at[sp, j], ysend.at[2, j], yrecv.at[2, j], {"sp": core}),
                remote(yall.at[across, j], yall.at[across, j], ysend.at[3, j], yrecv.at[3, j], {"sp": core}))

    for j in range(NOC):
        y = jnp.zeros((B, OCH), jnp.float32)
        for i in range(half):
            y = y + jnp.dot(lhs[i], wbuf[i * 2 * HD:(i + 1) * 2 * HD, j * OCH:(j + 1) * OCH],
                            preferred_element_type=jnp.float32)
        ypart[j] = y
        piece(j)[0].start()
    for j in range(NOC):
        p = piece(j)
        p[0].wait_recv()
        yall[sp, j] = ypart[j] + yin[j]
        p[1].start()
        p[2].start()
    for j in range(NOC):
        p = piece(j)
        p[1].wait_recv()
        p[3].start()
    for j in range(NOC):
        p = piece(j)
        p[2].wait_recv()
        p[3].wait_recv()
        for i in range(4):
            p[i].wait_send()
    for s in range(4):
        for j in range(NOC):
            at = s * OC + j * OCH
            out_ref[:, at:at + OCH] = (h_ref[:, at:at + OCH].astype(jnp.float32) + yall[s, j]).astype(jnp.bfloat16)
    for c in (c1, c2, c3, *mlc):
        c.wait_send()


def solution(mesh):
    half_dim = HD // 2
    freq = 1.0 / (ROPE_BASE ** (np.arange(half_dim, dtype=np.float64) * 2.0 / HD))
    freq = np.concatenate([freq, freq]).astype(np.float32)[None, :]

    def local_step(hidden, norm_gain, w_query, w_key, w_value, w_out, k_cache, v_cache, positions):
        f32, bf16 = jnp.float32, jnp.bfloat16
        dma = pltpu.SemaphoreType.DMA
        g = pl.pallas_call(
            qkv_kernel,
            out_shape=jax.ShapeDtypeStruct((3, HL * B, HD), f32),
            in_specs=[SMEM, VMEM, VMEM, VMEM, ANY, ANY, ANY],
            out_specs=VMEM,
            scratch_shapes=[pltpu.VMEM((3, D, CW), bf16), pltpu.VMEM((B, D), bf16), pltpu.VMEM((3, HL * B, HD), f32),
                            dma((3, NKC)), dma((3, 3)), dma((3, 3))],
            compiler_params=pltpu.CompilerParams(collective_id=0, has_side_effects=True, vmem_limit_bytes=40 << 20),
            name="qkv",
        )(positions, hidden, norm_gain[None, :], jnp.asarray(freq), w_query, w_key, w_value)

        kt = jnp.transpose(k_cache, (0, 2, 1, 3))
        vt = jnp.transpose(v_cache, (0, 2, 1, 3))
        ko, vo, acc, ml = pl.pallas_call(
            cache_kernel,
            out_shape=(jax.ShapeDtypeStruct(kt.shape, bf16), jax.ShapeDtypeStruct(vt.shape, bf16),
                       jax.ShapeDtypeStruct((HL * B, HD), f32), jax.ShapeDtypeStruct((HL, HD), f32)),
            in_specs=[SMEM, VMEM, ANY, ANY],
            out_specs=(ANY, ANY, VMEM, VMEM),
            scratch_shapes=[pltpu.VMEM((SLOTS, HL, SL, HD), bf16), pltpu.VMEM((SLOTS, HL, SL, HD), bf16),
                            pltpu.VMEM((2, HL, SL), f32), dma((2, SLOTS)), dma((2, SLOTS))],
            compiler_params=pltpu.CompilerParams(vmem_limit_bytes=48 << 20),
            name="cache",
        )(positions, g, kt, vt)

        hr = HL // 2 * B
        out = pl.pallas_call(
            out_kernel,
            out_shape=jax.ShapeDtypeStruct((B, D), bf16),
            in_specs=[VMEM, VMEM, VMEM, ANY],
            out_specs=VMEM,
            scratch_shapes=[pltpu.VMEM((HL * HD, OC), bf16), pltpu.VMEM((4, HL, HD), f32),
                            pltpu.VMEM((hr, HD), f32), pltpu.VMEM((hr, HD), f32), pltpu.VMEM((hr, HD), f32),
                            pltpu.VMEM((hr, HD), f32), pltpu.VMEM((HL * B, HD), f32),
                            pltpu.VMEM((NOC, B, OCH), f32), pltpu.VMEM((NOC, B, OCH), f32),
                            pltpu.VMEM((4, NOC, B, OCH), f32),
                            dma((HL * HD // KC,)), dma((3,)), dma((3,)), dma((3,)), dma((3,)),
                            dma((4, NOC)), dma((4, NOC))],
            compiler_params=pltpu.CompilerParams(collective_id=1, has_side_effects=True, vmem_limit_bytes=32 << 20),
            name="out",
        )(acc, ml, hidden, w_out)
        return out, jnp.transpose(ko, (0, 2, 1, 3)), jnp.transpose(vo, (0, 2, 1, 3))

    cache_spec = P("dp", "sp", "tp", None)
    specs_in = (P("dp", None), P(None), P(None, "tp"), P(None, "tp"), P(None, "tp"), P("tp", None), cache_spec, cache_spec, P("dp"))
    specs_out = (P("dp", None), cache_spec, cache_spec)
    return jax.shard_map(local_step, mesh=mesh, in_specs=specs_in, out_specs=specs_out, check_vma=False)
```

time: 214 us -> 98.1 us (0.46)
  Pallas kernels: 0 us -> 93.5 us
  matrix products: 79.5 us -> 0 us
  other arithmetic: 68.1 us -> 0 us
  waiting for transfers between devices: 51.2 us -> 0 us
  between operations: 14.2 us -> 0.7 us
  local copies, waits for them, and re-layouts: 0.92 us -> 3.75 us
    pallas_call x0 -> x3, Pallas kernels: none -> 93.5 us  [the longest x1 56.3 us: local_step(): pl.pallas_call(cache_kernel, out_shape=(jax.ShapeDtypeStruct(kt.shape, bf...]
    dot_general x6 -> x0, matrix products: 79.5 us -> none  [the longest x1 16.8 us: local_step(): jnp.einsum('bkgd,bskd->bkgs', q_rot, k_updated, preferred_element_type=jn...]
    select_n x1 -> x0, other arithmetic: 55 us -> none  [local_step(): v_updated = jnp.where(slot_mask, v_new[:, None], v_cache)]
    psum x1 -> x0, waiting for transfers between devices: 25.9 us -> none  [local_step(): proj_out = lax.psum(part_proj, 'tp')]
    all_gather x1 -> x0, waiting for transfers between devices: 25.4 us -> none  [local_step(): gathered = lax.all_gather(block_stats, 'sp')]
    unnamed x4 -> x13, local copies, waits for them, and re-layouts: 0.01 us -> 3.75 us
    reduce_sum x2 -> x0, other arithmetic: 2.9 us -> none  [the longest x1 1.76 us: local_step(): total_acc = jnp.sum(gathered[..., :head_dim] * rescale, axis=0)]
    convert_element_type x3 -> x0, other arithmetic: 2.9 us -> none  [the longest x1 1.87 us: local_step(): return ((resid_f32 + proj_out).astype(jnp.bfloat16), k_updated, v_updated)]
  transfers between devices with their start and end apart: 2 -> 0, of which waited for: 2 -> 0; matrix products, arithmetic and copies ran while one was open for 0% -> 0% of each run, Pallas kernels for 0% -> 0%
where the time goes in v1:
time: 98.1 us; the launch traced here: 98 us
  Pallas kernels  93.5 us (95%)
  local copies, waits for them, and re-layouts  3.75 us (4%)
    pallas_call x1, Pallas kernels, local_step(): pl.pallas_call(cache_kernel, out_shape=(jax.ShapeDtypeStruct(kt.shape, bf...  56.3 us
    pallas_call x1, Pallas kernels, local_step(): pl.pallas_call(out_kernel, out_shape=jax.ShapeDtypeStruct((B, D), bf16),...  20.3 us
    pallas_call x1, Pallas kernels, local_step(): pl.pallas_call(qkv_kernel, out_shape=jax.ShapeDtypeStruct((3, HL * B, HD)...  16.9 us
    unnamed x13, local copies, waits for them, and re-layouts  3.75 us

profile of v1, /device:TPU:0, one launch (start us, length us, event | category | flops | bytes accessed | tf_op | source)
XLA Modules:
  0.0 98.0 jit_solution(5524647626185174387)
XLA Ops:
  0.6 0.0 copy-start.4
  0.6 0.0 copy-start
  0.7 1.0 copy-done
  1.6 0.0 copy-start.2
  1.6 0.7 copy-done.2
  2.3 0.0 copy-start.3
  2.4 0.7 copy-done.3
  3.0 0.0 copy-start.5
  3.0 0.7 copy-done.5
  3.7 16.9 %qkv.1.g_ref = f32[3,640,128]{2,1,0:T(8,128)S(1)} custom-call(s32[32]{0:T(128)S(1)} %copy-done.3, bf16[32,5120]{1,0:T(8,128)(2,1)S(1)} %copy-done, f32[1,5120]{1,0:T(1,128)S(1)} %bitcast.5, f32[1,128]{1,0:T(1,128)S(1)} %copy-done.5, bf16[5120,2560]{1,0:T(8,128)(2,1)} %wq_ref.1, bf16[5120,2560]{1,0:T(8,128)(2,1)} %wk_ref.1, bf16[5120,2560]{1,0:T(8,128)(2,1)} %wv_ref.1), custom_call_target="tpu_custom_call" | custom-call | tf_op jit(solution)/shard_map/qkv/pallas_call | solution.py:328
  20.5 0.0 copy-done.4
  20.5 0.0 copy-start.1
  20.6 56.3 %cache.1 = (bf16[32,20,256,128]{3,2,1,0:T(8,128)(2,1)}, bf16[32,20,256,128]{3,2,1,0:T(8,128)(2,1)}, f32[640,128]{1,0:T(8,128)S(1)}, f32[20,128]{1,0:T(8,128)S(1)}) custom-call(s32[32]{0:T(128)S(1)} %copy-done.4, f32[3,640,128]{2,1,0:T(8,128)S(1)} %qkv.1.g_ref, bf16[32,20,256,128]{3,2,1,0:T(8,128)(2,1)} %bitcast.6, bf16[32,20,256,128]{3,2,1,0:T(8,128)(2,1)} %bitcast.7), custom_call_target="tpu_custom_call" | custom-call | tf_op jit(solution)/shard_map/cache/pallas_call | solution.py:341
  76.9 0.0 copy-done.1
  76.9 20.3 %out.1 = bf16[32,5120]{1,0:T(8,128)(2,1)S(1)} custom-call(f32[640,128]{1,0:T(8,128)S(1)} %get-tuple-element.7.acc_ref, f32[20,128]{1,0:T(8,128)S(1)} %get-tuple-element.8.ml_ref, bf16[32,5120]{1,0:T(8,128)(2,1)S(1)} %copy-done.1, bf16[2560,5120]{1,0:T(8,128)(2,1)} %w_ref.1), custom_call_target="tpu_custom_call" | custom-call | tf_op jit(solution)/shard_map/out/pallas_call | solution.py:354
  97.2 0.7 copy.14
Async XLA Ops:
  0.6 19.9 %copy-start.4 = (s32[32]{0:T(128)S(1)}, s32[32]{0:T(128)}, u32[]{:S(2)}) copy-start(s32[32]{0:T(128)} %pos_ref.3) | copy-start | bytes 388
  0.6 1.0 copy-start
  1.6 0.7 copy-start.2
  2.3 0.7 copy-start.3
  3.0 0.7 copy-start.5
  20.5 56.4 %copy-start.1 = (bf16[32,5120]{1,0:T(8,128)(2,1)S(1)}, bf16[32,5120]{1,0:T(8,128)(2,1)}, u32[]{:S(2)}) copy-start(bf16[32,5120]{1,0:T(8,128)(2,1)} %h_ref.3) | copy-start | bytes 983044

commit v2 on v0

v2 whole, which is shorter than its diff:
```python
import jax
import jax.numpy as jnp
import numpy as np
from jax import lax
from jax.experimental import pallas as pl
from jax.experimental.pallas import tpu as pltpu
from jax.sharding import PartitionSpec as P

ROPE_BASE = 1000000.0
EPS = 1e-5
NEG_BIG = -1e30
MESH = pl.DeviceIdType.MESH
VMEM = pl.BlockSpec(memory_space=pltpu.VMEM)
SMEM = pl.BlockSpec(memory_space=pltpu.SMEM)

B = 32
D = 5120
HL = 20
HD = 128
SL = 256
HS = 5
CW = HS * HD
KC = 1280
NKC = D // KC
OC = 1280
OCH = 256
NOC = OC // OCH
OK = 512
NB = 8
NA = B - NB
SLOTS = 9
EARLY = 8
AHEAD = 5
SCALE = HD ** -0.5
HBM = pl.BlockSpec(memory_space=pltpu.HBM)


def peers():
    sp = lax.axis_index("sp")
    across = lax.rem(sp + 2, 4)
    core = sp + 1 - 2 * lax.rem(sp, 2)
    return sp, across, core


def remote(src, dst, send, recv, dev):
    return pltpu.make_async_remote_copy(src_ref=src, dst_ref=dst, send_sem=send, recv_sem=recv,
                                        device_id=dev, device_id_type=MESH)


def qkv_kernel(pos_hbm, h_hbm, gain_hbm, freq_hbm, wq_ref, wk_ref, wv_ref, k_ref, v_ref, out_ref, kring, vring,
               wbuf, xn, g, pos_ref, h_ref, gain_ref, freq_ref, insem, wsem, ssem, rsem, tsem):
    sp, across, core = peers()
    bar = pltpu.get_barrier_semaphore()
    for dev in (across, core):
        pl.semaphore_signal(bar, inc=1, device_id={"sp": dev}, device_id_type=MESH)
    cols = pl.ds(pl.multiple_of(sp * CW, HD), CW)
    small = [pltpu.make_async_copy(src, dst, insem.at[i]) for i, (src, dst) in enumerate(
        ((h_hbm, h_ref), (gain_hbm, gain_ref), (freq_hbm, freq_ref), (pos_hbm, pos_ref)))]
    for c in small:
        c.start()

    def chunk(kind, c):
        src = (wq_ref, wk_ref, wv_ref)[kind]
        rows = pl.ds(c * KC, KC)
        return pltpu.make_async_copy(src.at[rows, cols], wbuf.at[kind, rows], wsem.at[kind, c])

    chunks = [[chunk(kind, c) for c in range(NKC)] for kind in range(3)]
    for kind in range(3):
        for c in chunks[kind]:
            c.start()
    tiles = [pltpu.make_async_copy(src.at[b], dst.at[b], tsem.at[i, b])
             for b in range(EARLY) for i, (src, dst) in enumerate(((k_ref, kring), (v_ref, vring)))]

    for c in small:
        c.wait()
    x = h_ref[...].astype(jnp.float32)
    inv = lax.rsqrt(jnp.mean(x * x, axis=-1, keepdims=True) + EPS)
    xn[...] = (x * inv * gain_ref[...]).astype(jnp.bfloat16)
    row = lax.broadcasted_iota(jnp.int32, (B, HD), 0)
    lane = lax.broadcasted_iota(jnp.int32, (B, HD), 1)
    pos = jnp.zeros((B, HD), jnp.int32)
    for b in range(B):
        pos = jnp.where(row == b, pos_ref[b], pos)
    angles = pos.astype(jnp.float32) * freq_ref[...]
    cosine = jnp.cos(angles)
    sine = jnp.sin(angles)
    sine = jnp.where(lane < HD // 2, -sine, sine)
    pl.semaphore_wait(bar, 2)

    own = pl.ds(pl.multiple_of(sp * HS * B, B), HS * B)
    far = pl.ds(pl.multiple_of(across * HS * B, B), HS * B)
    links = [(remote(g.at[kind, own], g.at[kind, own], ssem.at[kind, 0], rsem.at[kind, 0], {"sp": across}),
              remote(g.at[kind, own], g.at[kind, own], ssem.at[kind, 1], rsem.at[kind, 1], {"sp": core}),
              remote(g.at[kind, far], g.at[kind, far], ssem.at[kind, 2], rsem.at[kind, 2], {"sp": core}))
             for kind in range(3)]

    for kind in range(3):
        acc = jnp.zeros((B, CW), jnp.float32)
        for c in range(NKC):
            chunks[kind][c].wait()
            rows = slice(c * KC, (c + 1) * KC)
            acc = acc + jnp.dot(xn[:, rows], wbuf[kind, rows, :], preferred_element_type=jnp.float32)
        for i in range(HS):
            u = acc[:, i * HD:(i + 1) * HD]
            if kind < 2:
                u = u * cosine + pltpu.roll(u, HD // 2, 1) * sine
            g[kind, pl.ds(pl.multiple_of(sp * HS * B + i * B, B), B), :] = u.astype(jnp.bfloat16).astype(jnp.float32)
        links[kind][0].start()
        links[kind][1].start()
        if kind > 0:
            links[kind - 1][0].wait_recv()
            links[kind - 1][2].start()
        if kind == 1:
            for c in tiles:
                c.start()
    links[2][0].wait_recv()
    links[2][2].start()
    for kind in range(3):
        links[kind][0].wait_send()
        links[kind][1].wait()
        links[kind][2].wait()
    out_ref[...] = g[...]
    for c in tiles:
        c.wait()


def row_of(rows, h, x):
    return jnp.where(rows == h, x, 0.0).astype(jnp.bfloat16)


def scores(q, keys):
    rows = lax.broadcasted_iota(jnp.int32, (HL, HD), 0)
    s = jnp.zeros((HL, SL), jnp.float32)
    for h in range(HL):
        s = s + lax.dot_general(row_of(rows, h, q), keys(h), (((1,), (1,)), ((), ())), preferred_element_type=jnp.float32)
    return s * SCALE


def weighted(p, values):
    rows = lax.broadcasted_iota(jnp.int32, (HL, SL), 0)
    o = jnp.zeros((HL, HD), jnp.float32)
    for h in range(HL):
        o = o + jnp.dot(row_of(rows, h, p), values(h), preferred_element_type=jnp.float32)
    return o


def insert_row(g_ref, b, at, tile_refs):
    @pl.when((at >= 0) & (at < SL))
    def _():
        start = pl.multiple_of((at // 16) * 16, 16)
        hit = lax.broadcasted_iota(jnp.int32, (16, HD), 0) == at - start
        for kind, buf, slot in tile_refs:
            for h in range(HL):
                new = jnp.broadcast_to(g_ref[kind, pl.ds(h * B + b, 1), :], (16, HD))
                old = buf[slot, h, pl.ds(start, 16), :].astype(jnp.float32)
                buf[slot, h, pl.ds(start, 16), :] = jnp.where(hit, new, old).astype(jnp.bfloat16)


def put_stats(ml_ref, b, m, total):
    lane = lax.broadcasted_iota(jnp.int32, (HL, HD), 1)
    ml_ref[...] = jnp.where(lane == b, m, jnp.where(lane == b + B, total, ml_ref[...]))


def cache_kernel(pos_ref, g_ref, k_ref, v_ref, kin, vin, ko_ref, vo_ref, acc_ref, ml_ref, kbuf, vbuf,
                 sbuf, rsem, wsem):
    del kin, vin
    base = lax.axis_index("sp") * SL

    def reads(b):
        slot = lax.rem(b, SLOTS)
        return (pltpu.make_async_copy(k_ref.at[b], kbuf.at[slot], rsem.at[0, slot]),
                pltpu.make_async_copy(v_ref.at[b], vbuf.at[slot], rsem.at[1, slot]))

    def write_k(b):
        slot = lax.rem(b, SLOTS)
        return pltpu.make_async_copy(kbuf.at[slot], ko_ref.at[b], wsem.at[0, slot])

    def write_v(b):
        slot = lax.rem(b, SLOTS)
        return pltpu.make_async_copy(vbuf.at[slot], vo_ref.at[b], wsem.at[1, slot])

    for b in range(EARLY, SLOTS):
        for c in reads(b):
            c.start()
    ml_ref[...] = jnp.zeros_like(ml_ref)

    def arrive(b):
        @pl.when(b >= EARLY)
        def _():
            for c in reads(b):
                c.wait()
        slot = lax.rem(b, SLOTS)
        insert_row(g_ref, b, pos_ref[b] - base, ((1, kbuf, slot), (2, vbuf, slot)))

    pcol = lax.broadcasted_iota(jnp.int32, (HL, SL), 1)

    def score(b):
        slot = lax.rem(b, SLOTS)
        sbuf[lax.rem(b, 2)] = scores(g_ref[0, pl.ds(b, HL, stride=B), :], lambda h: kbuf[slot, h])

    def value(b):
        slot = lax.rem(b, SLOTS)
        valid = pcol <= pos_ref[b] - base
        s = jnp.where(valid, sbuf[lax.rem(b, 2)], NEG_BIG)
        m = jnp.max(s, axis=-1, keepdims=True)
        p = jnp.where(valid, jnp.exp(s - m), 0.0)
        total = jnp.sum(p, axis=-1, keepdims=True)
        acc_ref[pl.ds(b, HL, stride=NA), :] = weighted(p, lambda h: vbuf[slot, h])
        put_stats(ml_ref, b, m, total)

    def ahead(b):
        @pl.when((b + AHEAD >= SLOTS) & (b + AHEAD < NA))
        def _():
            write_k(b + AHEAD - SLOTS).wait()
            write_v(b + AHEAD - SLOTS).wait()
            for c in reads(b + AHEAD):
                c.start()

    arrive(0)
    ahead(0)
    score(0)
    write_k(0).start()

    @pl.loop(1, NA)
    def _(b):
        arrive(b)
        ahead(b)
        score(b)
        value(b - 1)
        write_k(b).start()
        write_v(b - 1).start()

    value(NA - 1)
    write_v(NA - 1).start()
    for b in range(NA - SLOTS, NA):
        write_k(b).wait()
        write_v(b).wait()


def tail_kernel(pos_ref, g_ref, acc_a, ml_a, h_ref, k_ref, v_ref, w_ref, out_ref, kt, vt,
                wbuf, sbuf, acc_b, ml_b, *scratch):
    sp, across, core = peers()
    diag = 3 - sp
    tp = lax.axis_index("tp")
    c01 = lax.rem(sp, 2)
    base = sp * SL
    half = HL // 2
    rsem, wsem = scratch[:2]
    bar = pltpu.get_barrier_semaphore()
    for dev in (across, core, diag):
        pl.semaphore_signal(bar, inc=1, device_id={"sp": dev}, device_id_type=MESH)
    pl.semaphore_signal(bar, inc=1, device_id={"tp": 1 - tp}, device_id_type=MESH)

    def reads(t):
        return (pltpu.make_async_copy(k_ref.at[NA + t], kt.at[t], rsem.at[0, t]),
                pltpu.make_async_copy(v_ref.at[NA + t], vt.at[t], rsem.at[1, t]))

    for t in range(NB):
        for c in reads(t):
            c.start()
    wcopies = [pltpu.make_async_copy(w_ref.at[pl.ds(i * OK, OK), pl.ds(pl.multiple_of(sp * OC, HD), OC)],
                                     wbuf.at[pl.ds(i * OK, OK)], wsem.at[i]) for i in range(HL * HD // OK)]
    for c in wcopies:
        c.start()

    def columns(table):
        t = jnp.where(c01 == 0, table[:half], table[half:])
        t = jnp.concatenate([t, jnp.zeros((HD - half, HD), jnp.float32)], axis=0)
        return jnp.transpose(t)

    class Rows:
        def __init__(self, n, first, acc, ml, bufs):
            self.n, self.first, self.acc, self.ml = n, first, acc, ml
            (self.mlbuf, self.r1, self.pair, self.r2, self.oall, self.ypart, self.yin, self.yall,
             mls, mlr, s, r, ys, yr) = bufs
            hr = half * n
            mine = pl.ds(pl.multiple_of(c01 * hr, 8), hr)
            theirs = pl.ds(pl.multiple_of((1 - c01) * hr, 8), hr)
            self.mlc = [remote(self.mlbuf.at[0], self.mlbuf.at[i + 1], mls.at[i], mlr.at[i], {"sp": dev})
                        for i, dev in enumerate((core, across, diag))]
            self.c1 = remote(acc.at[theirs], self.r1, s.at[0], r.at[0], {"sp": core})
            self.c2 = remote(self.pair, self.r2, s.at[1], r.at[1], {"sp": across})
            self.c3 = remote(self.oall.at[mine], self.oall.at[mine], s.at[2], r.at[2], {"sp": core})
            ya = self.yall
            self.pieces = [(remote(self.ypart.at[j], self.yin.at[j], ys.at[0, j], yr.at[0, j], {"tp": 1 - tp}),
                            remote(ya.at[sp, j], ya.at[sp, j], ys.at[1, j], yr.at[1, j], {"sp": across}),
                            remote(ya.at[sp, j], ya.at[sp, j], ys.at[2, j], yr.at[2, j], {"sp": core}),
                            remote(ya.at[across, j], ya.at[across, j], ys.at[3, j], yr.at[3, j], {"sp": core}))
                           for j in range(NOC)]

        def mine(self, i):
            return pl.ds(pl.multiple_of((c01 * half + i) * self.n, 8), self.n)

        def start(self):
            self.mlbuf[0] = self.ml[...]
            self.mlc[0].start()
            self.c1.start()
            self.mlc[1].start()
            self.mlc[2].start()

        def merge_core(self):
            n = self.n
            self.mlc[0].wait_recv()
            own, other = self.mlbuf[0], self.mlbuf[1]
            m_pair = jnp.maximum(own, other)
            f_own, f_other = columns(jnp.exp(own - m_pair)), columns(jnp.exp(other - m_pair))
            self.c1.wait_recv()
            for i in range(half):
                rows = slice(i * n, (i + 1) * n)
                self.pair[rows, :] = (self.acc[self.mine(i), :] * f_own[self.first:self.first + n, i:i + 1]
                                      + self.r1[rows, :] * f_other[self.first:self.first + n, i:i + 1])
            self.c2.start()

        def merge_across(self):
            n = self.n
            self.mlc[1].wait_recv()
            self.mlc[2].wait_recv()
            tabs = [self.mlbuf[i] for i in range(4)]
            m_pair, m_far = jnp.maximum(tabs[0], tabs[1]), jnp.maximum(tabs[2], tabs[3])
            m_all = jnp.maximum(m_pair, m_far)
            total = jnp.zeros((HL, HD), jnp.float32)
            for t in tabs:
                total = total + jnp.exp(t - m_all) * pltpu.roll(t, HD - B, 1)
            lane = lax.broadcasted_iota(jnp.int32, (HL, HD), 1)
            live = (lane >= self.first) & (lane < self.first + n)
            total = jnp.where(live, total, 1.0)
            g_pair, g_far = columns(jnp.exp(m_pair - m_all) / total), columns(jnp.exp(m_far - m_all) / total)
            self.c2.wait_recv()
            for i in range(half):
                rows = slice(i * n, (i + 1) * n)
                self.oall[self.mine(i), :] = (self.pair[rows, :] * g_pair[self.first:self.first + n, i:i + 1]
                                              + self.r2[rows, :] * g_far[self.first:self.first + n, i:i + 1])
            self.c3.start()

        def project(self):
            n = self.n
            self.c3.wait_recv()
            lhs = [jnp.concatenate([self.oall[2 * i * n:(2 * i + 1) * n, :], self.oall[(2 * i + 1) * n:(2 * i + 2) * n, :]],
                                   axis=1).astype(jnp.bfloat16) for i in range(half)]
            for j in range(NOC):
                y = jnp.zeros((n, OCH), jnp.float32)
                for i in range(half):
                    y = y + jnp.dot(lhs[i], wbuf[i * 2 * HD:(i + 1) * 2 * HD, j * OCH:(j + 1) * OCH],
                                    preferred_element_type=jnp.float32)
                self.ypart[j] = y
                self.pieces[j][0].start()

        def total(self):
            for j in range(NOC):
                self.pieces[j][0].wait_recv()
                self.yall[sp, j] = self.ypart[j] + self.yin[j]
                self.pieces[j][1].start()
                self.pieces[j][2].start()

        def forward(self):
            for j in range(NOC):
                self.pieces[j][1].wait_recv()
                self.pieces[j][3].start()

        def finish(self):
            for j in range(NOC):
                self.pieces[j][2].wait_recv()
                self.pieces[j][3].wait_recv()
            rows = slice(self.first, self.first + self.n)
            for s in range(4):
                for j in range(NOC):
                    at = slice(s * OC + j * OCH, s * OC + (j + 1) * OCH)
                    out_ref[rows, at] = (h_ref[rows, at].astype(jnp.float32) + self.yall[s, j]).astype(jnp.bfloat16)
            for c in (self.c1, self.c2, self.c3, *self.mlc, *(p for ps in self.pieces for p in ps)):
                c.wait_send()

    rest = scratch[2:]
    first = Rows(NA, 0, acc_a, ml_a, rest[:14])
    last = Rows(NB, NA, acc_b, ml_b, rest[14:])
    ml_b[...] = jnp.zeros_like(ml_b)
    pl.semaphore_wait(bar, 4)
    first.start()

    pcol = lax.broadcasted_iota(jnp.int32, (HL, SL), 1)

    def arrive(t):
        for c in reads(t):
            c.wait()

    def score(t):
        sbuf[lax.rem(t, 2)] = scores(g_ref[0, pl.ds(NA + t, HL, stride=B), :], lambda h: kt[t, h])

    def value(t):
        b = NA + t
        at = jnp.full((HL, 1), pos_ref[b] - base)
        here = (at >= 0) & (at < SL)
        q, k_new, v_new = (g_ref[i, pl.ds(b, HL, stride=B), :] for i in range(3))
        s_new = jnp.where(here, jnp.sum(q * k_new, axis=-1, keepdims=True) * SCALE, NEG_BIG)
        valid = pcol < at
        s = jnp.where(valid, sbuf[lax.rem(t, 2)], NEG_BIG)
        m = jnp.maximum(jnp.max(s, axis=-1, keepdims=True), s_new)
        p = jnp.where(valid, jnp.exp(s - m), 0.0)
        p_new = jnp.where(here, jnp.exp(s_new - m), 0.0)
        total = jnp.sum(p, axis=-1, keepdims=True) + p_new
        o = weighted(p, lambda h: vt[t, h]) + p_new.astype(jnp.bfloat16).astype(jnp.float32) * v_new
        acc_b[pl.ds(t, HL, stride=NB), :] = o
        put_stats(ml_b, b, m, total)

    arrive(0)
    score(0)

    @pl.loop(1, NB)
    def _(t):
        arrive(t)
        score(t)
        value(t - 1)

        @pl.when(t == 2)
        def _():
            first.merge_core()

        @pl.when(t == 6)
        def _():
            first.merge_across()

    value(NB - 1)
    last.start()
    for c in wcopies:
        c.wait()
    first.project()
    last.merge_core()
    last.merge_across()
    first.total()
    last.project()
    first.forward()
    last.total()
    first.finish()
    last.forward()
    last.finish()


def write_kernel(pos_ref, g_ref, kin, vin, koin, voin, ko_ref, vo_ref, kt, vt, wsem):
    del kin, vin, koin, voin
    base = lax.axis_index("sp") * SL

    def writes(t):
        return (pltpu.make_async_copy(kt.at[t], ko_ref.at[NA + t], wsem.at[0, t]),
                pltpu.make_async_copy(vt.at[t], vo_ref.at[NA + t], wsem.at[1, t]))

    @pl.loop(0, NB)
    def _(t):
        insert_row(g_ref, NA + t, pos_ref[NA + t] - base, ((1, kt, t), (2, vt, t)))
        for c in writes(t):
            c.start()

    @pl.loop(0, NB)
    def _(t):
        for c in writes(t):
            c.wait()


def solution(mesh):
    half_dim = HD // 2
    freq = 1.0 / (ROPE_BASE ** (np.arange(half_dim, dtype=np.float64) * 2.0 / HD))
    freq = np.concatenate([freq, freq]).astype(np.float32)[None, :]
    f32, bf16 = jnp.float32, jnp.bfloat16
    dma = pltpu.SemaphoreType.DMA

    def shape(dims, dtype):
        return jax.ShapeDtypeStruct(dims, dtype)

    def exchange(n):
        hr = HL // 2 * n
        return [pltpu.VMEM((4, HL, HD), f32), pltpu.VMEM((hr, HD), f32), pltpu.VMEM((hr, HD), f32), pltpu.VMEM((hr, HD), f32),
                pltpu.VMEM((2 * hr, HD), f32), pltpu.VMEM((NOC, n, OCH), f32), pltpu.VMEM((NOC, n, OCH), f32),
                pltpu.VMEM((4, NOC, n, OCH), f32), dma((3,)), dma((3,)), dma((3,)), dma((3,)), dma((4, NOC)), dma((4, NOC))]

    def local_step(hidden, norm_gain, w_query, w_key, w_value, w_out, k_cache, v_cache, positions):
        kt = jnp.transpose(k_cache, (0, 2, 1, 3))
        vt = jnp.transpose(v_cache, (0, 2, 1, 3))
        ring = pltpu.VMEM((SLOTS, HL, SL, HD), bf16)
        g, kring, vring = pl.pallas_call(
            qkv_kernel,
            out_shape=(shape((3, HL * B, HD), f32), ring, ring),
            in_specs=[HBM] * 9,
            out_specs=(VMEM, VMEM, VMEM),
            scratch_shapes=[pltpu.VMEM((3, D, CW), bf16), pltpu.VMEM((B, D), bf16), pltpu.VMEM((3, HL * B, HD), f32),
                            pltpu.SMEM((B,), jnp.int32), pltpu.VMEM((B, D), bf16), pltpu.VMEM((1, D), f32),
                            pltpu.VMEM((1, HD), f32), dma((4,)), dma((3, NKC)), dma((3, 3)), dma((3, 3)), dma((2, EARLY))],
            compiler_params=pltpu.CompilerParams(collective_id=0, has_side_effects=True, vmem_limit_bytes=26 << 20),
            name="qkv",
        )(*(pltpu.with_memory_space_constraint(x, pltpu.HBM) for x in (
            positions, hidden, norm_gain[None, :], jnp.asarray(freq), w_query, w_key, w_value, kt, vt)))

        ko, vo, acc, ml, _, _ = pl.pallas_call(
            cache_kernel,
            out_shape=(shape(kt.shape, bf16), shape(vt.shape, bf16), shape((HL * NA, HD), f32), shape((HL, HD), f32), ring, ring),
            in_specs=[SMEM, VMEM, HBM, HBM, VMEM, VMEM],
            out_specs=(HBM, HBM, VMEM, VMEM, VMEM, VMEM),
            scratch_shapes=[pltpu.VMEM((2, HL, SL), f32), dma((2, SLOTS)), dma((2, SLOTS))],
            input_output_aliases={4: 4, 5: 5},
            compiler_params=pltpu.CompilerParams(vmem_limit_bytes=8 << 20),
            name="cache",
        )(positions, g, kt, vt, kring, vring)

        tiles = pltpu.VMEM((NB, HL, SL, HD), bf16)
        out, kl, vl = pl.pallas_call(
            tail_kernel,
            out_shape=(shape((B, D), bf16), tiles, tiles),
            in_specs=[SMEM, VMEM, VMEM, VMEM, VMEM, HBM, HBM, HBM],
            out_specs=(VMEM, VMEM, VMEM),
            scratch_shapes=[pltpu.VMEM((HL * HD, OC), bf16), pltpu.VMEM((2, HL, SL), f32),
                            pltpu.VMEM((HL * NB, HD), f32), pltpu.VMEM((HL, HD), f32),
                            dma((2, NB)), dma((HL * HD // OK,)), *exchange(NA), *exchange(NB)],
            compiler_params=pltpu.CompilerParams(collective_id=1, has_side_effects=True, vmem_limit_bytes=18 << 20),
            name="tail",
        )(positions, g, acc, ml, hidden, kt, vt, w_out)

        ko, vo, _, _ = pl.pallas_call(
            write_kernel,
            out_shape=(shape(kt.shape, bf16), shape(vt.shape, bf16), tiles, tiles),
            in_specs=[SMEM, VMEM, VMEM, VMEM, HBM, HBM],
            out_specs=(HBM, HBM, VMEM, VMEM),
            scratch_shapes=[dma((2, NB))],
            input_output_aliases={2: 2, 3: 3, 4: 0, 5: 1},
            compiler_params=pltpu.CompilerParams(vmem_limit_bytes=8 << 20),
            name="write",
        )(positions, g, kl, vl, ko, vo)
        return out, jnp.transpose(ko, (0, 2, 1, 3)), jnp.transpose(vo, (0, 2, 1, 3))

    cache_spec = P("dp", "sp", "tp", None)
    specs_in = (P("dp", None), P(None), P(None, "tp"), P(None, "tp"), P(None, "tp"), P("tp", None), cache_spec, cache_spec, P("dp"))
    specs_out = (P("dp", None), cache_spec, cache_spec)
    return jax.shard_map(local_step, mesh=mesh, in_specs=specs_in, out_specs=specs_out, check_vma=False)
```

time: 214 us -> 94.1 us (0.44)
  Pallas kernels: 0 us -> 92.6 us
  matrix products: 79.5 us -> 0 us
  other arithmetic: 68.1 us -> 0 us
  waiting for transfers between devices: 51.2 us -> 0 us
  between operations: 14.2 us -> 0.7 us
    pallas_call x0 -> x4, Pallas kernels: none -> 92.6 us  [the longest x1 35.9 us: local_step(): pl.pallas_call(cache_kernel, out_shape=(shape(kt.shape, bf16), shape(vt.s...]
    dot_general x6 -> x0, matrix products: 79.5 us -> none  [the longest x1 16.8 us: local_step(): jnp.einsum('bkgd,bskd->bkgs', q_rot, k_updated, preferred_element_type=jn...]
    select_n x1 -> x0, other arithmetic: 55 us -> none  [local_step(): v_updated = jnp.where(slot_mask, v_new[:, None], v_cache)]
    psum x1 -> x0, waiting for transfers between devices: 25.9 us -> none  [local_step(): proj_out = lax.psum(part_proj, 'tp')]
    all_gather x1 -> x0, waiting for transfers between devices: 25.4 us -> none  [local_step(): gathered = lax.all_gather(block_stats, 'sp')]
    reduce_sum x2 -> x0, other arithmetic: 2.9 us -> none  [the longest x1 1.76 us: local_step(): total_acc = jnp.sum(gathered[..., :head_dim] * rescale, axis=0)]
    convert_element_type x3 -> x0, other arithmetic: 2.9 us -> none  [the longest x1 1.87 us: local_step(): return ((resid_f32 + proj_out).astype(jnp.bfloat16), k_updated, v_updated)]
    exp x1 -> x0, other arithmetic: 2.71 us -> none  [local_step(): rescale = jnp.exp(all_max - global_max)]
  transfers between devices with their start and end apart: 2 -> 0, of which waited for: 2 -> 0; matrix products, arithmetic and copies ran while one was open for 0% -> 0% of each run, Pallas kernels for 0% -> 0%
where the time goes in v2:
time: 94.1 us; the launch traced here: 94 us
  Pallas kernels  92.6 us (98%)
    pallas_call x1, Pallas kernels, local_step(): pl.pallas_call(cache_kernel, out_shape=(shape(kt.shape, bf16), shape(vt.s...  35.9 us
    pallas_call x1, Pallas kernels, local_step(): pl.pallas_call(tail_kernel, out_shape=(shape((B, D), bf16), tiles, tiles)...  27.9 us
    pallas_call x1, Pallas kernels, local_step(): pl.pallas_call(qkv_kernel, out_shape=(shape((3, HL * B, HD), f32), ring,...  20.9 us
    pallas_call x1, Pallas kernels, local_step(): pl.pallas_call(write_kernel, out_shape=(shape(kt.shape, bf16), shape(vt.s...  7.82 us

profile of v2, /device:TPU:0, one launch (start us, length us, event | category | flops | bytes accessed | tf_op | source)
XLA Modules:
  0.0 94.0 jit_solution(9926371128648349368)
XLA Ops:
  0.6 0.0 copy-start.1
  0.6 20.9 %qkv.1 = (f32[3,640,128]{2,1,0:T(8,128)S(1)}, bf16[9,20,256,128]{3,2,1,0:T(8,128)(2,1)S(1)}, bf16[9,20,256,128]{3,2,1,0:T(8,128)(2,1)S(1)}) custom-call(s32[32]{0:T(128)} %pos_ref.5, bf16[32,5120]{1,0:T(8,128)(2,1)} %h_ref.1, f32[1,5120]{1,0:T(1,128)} %bitcast.13, f32[1,128]{1,0:T(1,128)} %constant.2.clone.freq_hbm, bf16[5120,2560]{1,0:T(8,128)(2,1)} %wq_ref.1, ...), custom_call_target="tpu_custom_call" | custom-call | tf_op jit(solution)/shard_map/qkv/pallas_call | solution.py:477
  21.6 0.0 copy-done.1
  21.6 0.0 copy-start
  21.6 35.9 %cache.1 = (bf16[32,20,256,128]{3,2,1,0:T(8,128)(2,1)}, bf16[32,20,256,128]{3,2,1,0:T(8,128)(2,1)}, f32[480,128]{1,0:T(8,128)S(1)}, f32[20,128]{1,0:T(8,128)S(1)...) custom-call(s32[32]{0:T(128)S(1)} %copy-done.1, ...), custom_call_target="tpu_custom_call", output_to_operand_aliasing={{4}: (4, {}), {5}: (5, {})} | custom-call | tf_op jit(solution)/shard_map/cache/pallas_call | solution.py:490
  57.5 0.0 copy-done
  57.6 27.9 %tail.1 = (bf16[32,5120]{1,0:T(8,128)(2,1)S(1)}, bf16[8,20,256,128]{3,2,1,0:T(8,128)(2,1)S(1)}, bf16[8,20,256,128]{3,2,1,0:T(8,128)(2,1)S(1)}) custom-call(s32[32]{0:T(128)S(1)} %copy-done.1, f32[3,640,128]{2,1,0:T(8,128)S(1)} %get-tuple-element.15.g_ref, f32[480,128]{1,0:T(8,128)S(1)} %get-tuple-element.18.acc_a, f32[20,128]{1,0:T(8,128)S(1)} %get-tuple-element.19.ml_a, ...), custom_call_target="tpu_custom_call" | custom-call | tf_op jit(solution)/shard_map/tail/pallas_call | solution.py:502
  85.5 7.8 %write.1 = (bf16[32,20,256,128]{3,2,1,0:T(8,128)(2,1)}, bf16[32,20,256,128]{3,2,1,0:T(8,128)(2,1)}, bf16[8,20,256,128]{3,2,1,0:T(8,128)(2,1)S(1)}, bf16[8,20,256,128]{3,2,1,0:T(8,128)(2,1)S(1)}) custom-call(s32[32]{0:T(128)S(1)} %copy-done.1, ...), custom_call_target="tpu_custom_call", output_to_operand_aliasing={{2}: (2, {}), {3}: (3, {}), {0}: (4, {}), {1}: (5, {})} | custom-call | tf_op jit(solution)/shard_map/write/pallas_call | solution.py:514
  93.3 0.7 copy.26
Async XLA Ops:
  0.6 20.9 %copy-start.1 = (s32[32]{0:T(128)S(1)}, s32[32]{0:T(128)}, u32[]{:S(2)}) copy-start(s32[32]{0:T(128)} %pos_ref.5) | copy-start | bytes 388
  21.6 36.0 %copy-start = (bf16[32,5120]{1,0:T(8,128)(2,1)S(1)}, bf16[32,5120]{1,0:T(8,128)(2,1)}, u32[]{:S(2)}) copy-start(bf16[32,5120]{1,0:T(8,128)(2,1)} %h_ref.1) | copy-start | bytes 983044

commit v3 on v2

v3 whole, which is shorter than its diff:
```python
import jax
import jax.numpy as jnp
import numpy as np
from jax import lax
from jax.experimental import pallas as pl
from jax.experimental.pallas import tpu as pltpu
from jax.sharding import PartitionSpec as P

ROPE_BASE = 1000000.0
EPS = 1e-5
NEG_BIG = -1e30
MESH = pl.DeviceIdType.MESH
VMEM = pl.BlockSpec(memory_space=pltpu.VMEM)
SMEM = pl.BlockSpec(memory_space=pltpu.SMEM)

B = 32
D = 5120
HL = 20
HD = 128
SL = 256
HS = 5
CW = HS * HD
KC = 1280
NKC = D // KC
OC = 1280
OCH = 256
NOC = OC // OCH
OK = 512
GR = 16
NG = B // GR
SLOTS = 9
EARLY = 8
AHEAD = 5
WINDOW = 5
SCALE = HD ** -0.5
HBM = pl.BlockSpec(memory_space=pltpu.HBM)


def peers():
    sp = lax.axis_index("sp")
    across = lax.rem(sp + 2, 4)
    core = sp + 1 - 2 * lax.rem(sp, 2)
    return sp, across, core


def remote(src, dst, send, recv, dev):
    return pltpu.make_async_remote_copy(src_ref=src, dst_ref=dst, send_sem=send, recv_sem=recv,
                                        device_id=dev, device_id_type=MESH)


def qkv_kernel(pos_hbm, h_hbm, gain_hbm, freq_hbm, wq_ref, wk_ref, wv_ref, k_ref, v_ref, out_ref, kring, vring,
               wbuf, xn, g, pos_ref, h_ref, gain_ref, freq_ref, insem, wsem, ssem, rsem, tsem):
    sp, across, core = peers()
    bar = pltpu.get_barrier_semaphore()
    for dev in (across, core):
        pl.semaphore_signal(bar, inc=1, device_id={"sp": dev}, device_id_type=MESH)
    cols = pl.ds(pl.multiple_of(sp * CW, HD), CW)
    small = [pltpu.make_async_copy(src, dst, insem.at[i]) for i, (src, dst) in enumerate(
        ((h_hbm, h_ref), (gain_hbm, gain_ref), (freq_hbm, freq_ref), (pos_hbm, pos_ref)))]
    for c in small:
        c.start()

    def chunk(kind, c):
        src = (wq_ref, wk_ref, wv_ref)[kind]
        rows = pl.ds(c * KC, KC)
        return pltpu.make_async_copy(src.at[rows, cols], wbuf.at[kind, rows], wsem.at[kind, c])

    chunks = [chunk(kind, c) for kind in range(3) for c in range(NKC)]
    tiles = [pltpu.make_async_copy(src.at[b], dst.at[b], tsem.at[i, b])
             for b in range(EARLY) for i, (src, dst) in enumerate(((k_ref, kring), (v_ref, vring)))]
    queue = chunks + tiles
    for c in queue[:WINDOW]:
        c.start()

    for c in small:
        c.wait()
    x = h_ref[...].astype(jnp.float32)
    inv = lax.rsqrt(jnp.mean(x * x, axis=-1, keepdims=True) + EPS)
    xn[...] = (x * inv * gain_ref[...]).astype(jnp.bfloat16)
    row = lax.broadcasted_iota(jnp.int32, (B, HD), 0)
    lane = lax.broadcasted_iota(jnp.int32, (B, HD), 1)
    pos = jnp.zeros((B, HD), jnp.int32)
    for b in range(B):
        pos = jnp.where(row == b, pos_ref[b], pos)
    angles = pos.astype(jnp.float32) * freq_ref[...]
    cosine = jnp.cos(angles)
    sine = jnp.sin(angles)
    sine = jnp.where(lane < HD // 2, -sine, sine)
    pl.semaphore_wait(bar, 2)

    own = pl.ds(pl.multiple_of(sp * HS * B, B), HS * B)
    far = pl.ds(pl.multiple_of(across * HS * B, B), HS * B)
    links = [(remote(g.at[kind, own], g.at[kind, own], ssem.at[kind, 0], rsem.at[kind, 0], {"sp": across}),
              remote(g.at[kind, own], g.at[kind, own], ssem.at[kind, 1], rsem.at[kind, 1], {"sp": core}),
              remote(g.at[kind, far], g.at[kind, far], ssem.at[kind, 2], rsem.at[kind, 2], {"sp": core}))
             for kind in range(3)]

    for kind in range(3):
        acc = jnp.zeros((B, CW), jnp.float32)
        for c in range(NKC):
            step = kind * NKC + c
            chunks[step].wait()
            queue[step + WINDOW].start()
            rows = slice(c * KC, (c + 1) * KC)
            acc = acc + jnp.dot(xn[:, rows], wbuf[kind, rows, :], preferred_element_type=jnp.float32)
        for i in range(HS):
            u = acc[:, i * HD:(i + 1) * HD]
            if kind < 2:
                u = u * cosine + pltpu.roll(u, HD // 2, 1) * sine
            g[kind, pl.ds(pl.multiple_of(sp * HS * B + i * B, B), B), :] = u.astype(jnp.bfloat16).astype(jnp.float32)
        links[kind][0].start()
        links[kind][1].start()
        if kind > 0:
            links[kind - 1][0].wait_recv()
            links[kind - 1][2].start()
    for c in queue[len(chunks) + WINDOW:]:
        c.start()
    links[2][0].wait_recv()
    links[2][2].start()
    for kind in range(3):
        links[kind][0].wait_send()
        links[kind][1].wait()
        links[kind][2].wait()
    out_ref[...] = g[...]
    for c in tiles:
        c.wait()


def row_of(rows, h, x):
    return jnp.where(rows == h, x, 0.0).astype(jnp.bfloat16)


def scores(q, keys):
    rows = lax.broadcasted_iota(jnp.int32, (HL, HD), 0)
    s = jnp.zeros((HL, SL), jnp.float32)
    for h in range(HL):
        s = s + lax.dot_general(row_of(rows, h, q), keys(h), (((1,), (1,)), ((), ())), preferred_element_type=jnp.float32)
    return s * SCALE


def weighted(p, values):
    rows = lax.broadcasted_iota(jnp.int32, (HL, SL), 0)
    o = jnp.zeros((HL, HD), jnp.float32)
    for h in range(HL):
        o = o + jnp.dot(row_of(rows, h, p), values(h), preferred_element_type=jnp.float32)
    return o


def insert_row(g_ref, b, at, tile_refs):
    @pl.when((at >= 0) & (at < SL))
    def _():
        start = pl.multiple_of((at // 16) * 16, 16)
        hit = lax.broadcasted_iota(jnp.int32, (16, HD), 0) == at - start
        for kind, buf, slot in tile_refs:
            for h in range(HL):
                new = jnp.broadcast_to(g_ref[kind, pl.ds(h * B + b, 1), :], (16, HD))
                old = buf[slot, h, pl.ds(start, 16), :].astype(jnp.float32)
                buf[slot, h, pl.ds(start, 16), :] = jnp.where(hit, new, old).astype(jnp.bfloat16)


def put_stats(ml_ref, b, m, total):
    lane = lax.broadcasted_iota(jnp.int32, (HL, HD), 1)
    ml_ref[...] = jnp.where(lane == b, m, jnp.where(lane == b + B, total, ml_ref[...]))


def cache_kernel(pos_ref, g_ref, k_ref, v_ref, kin, vin, ko_ref, vo_ref, acc_ref, ml_ref, kbuf, vbuf,
                 sbuf, rsem, wsem):
    del kin, vin
    base = lax.axis_index("sp") * SL

    def reads(b):
        slot = lax.rem(b, SLOTS)
        return (pltpu.make_async_copy(k_ref.at[b], kbuf.at[slot], rsem.at[0, slot]),
                pltpu.make_async_copy(v_ref.at[b], vbuf.at[slot], rsem.at[1, slot]))

    def write_k(b):
        slot = lax.rem(b, SLOTS)
        return pltpu.make_async_copy(kbuf.at[slot], ko_ref.at[b], wsem.at[0, slot])

    def write_v(b):
        slot = lax.rem(b, SLOTS)
        return pltpu.make_async_copy(vbuf.at[slot], vo_ref.at[b], wsem.at[1, slot])

    for b in range(EARLY, SLOTS):
        for c in reads(b):
            c.start()
    ml_ref[...] = jnp.zeros_like(ml_ref)

    def arrive(b):
        @pl.when(b >= EARLY)
        def _():
            for c in reads(b):
                c.wait()
        slot = lax.rem(b, SLOTS)
        insert_row(g_ref, b, pos_ref[b] - base, ((1, kbuf, slot), (2, vbuf, slot)))

    pcol = lax.broadcasted_iota(jnp.int32, (HL, SL), 1)

    def score(b):
        slot = lax.rem(b, SLOTS)
        sbuf[lax.rem(b, 2)] = scores(g_ref[0, pl.ds(b, HL, stride=B), :], lambda h: kbuf[slot, h])

    def value(b):
        slot = lax.rem(b, SLOTS)
        valid = pcol <= pos_ref[b] - base
        s = jnp.where(valid, sbuf[lax.rem(b, 2)], NEG_BIG)
        m = jnp.max(s, axis=-1, keepdims=True)
        p = jnp.where(valid, jnp.exp(s - m), 0.0)
        total = jnp.sum(p, axis=-1, keepdims=True)
        acc_ref[b // GR, pl.ds(lax.rem(b, GR), HL, stride=GR), :] = weighted(p, lambda h: vbuf[slot, h])
        put_stats(ml_ref, b, m, total)

    def ahead(b):
        @pl.when((b + AHEAD >= SLOTS) & (b + AHEAD < B))
        def _():
            write_k(b + AHEAD - SLOTS).wait()
            write_v(b + AHEAD - SLOTS).wait()
            for c in reads(b + AHEAD):
                c.start()

    arrive(0)
    ahead(0)
    score(0)
    write_k(0).start()
    write_v(0).start()

    @pl.loop(1, B)
    def _(b):
        arrive(b)
        ahead(b)
        score(b)
        value(b - 1)
        write_k(b).start()
        write_v(b).start()

    value(B - 1)
    for b in range(B - SLOTS, B):
        write_k(b).wait()
        write_v(b).wait()


def out_kernel(acc_ref, ml_ref, h_ref, w_ref, out_ref,
               wbuf, mlbuf, r1, pair, r2, oall, ypart, yin, yall,
               wsem, mlsend, mlrecv, ssem, rsem, ysend, yrecv):
    sp, across, core = peers()
    diag = 3 - sp
    tp = lax.axis_index("tp")
    c01 = lax.rem(sp, 2)
    half = HL // 2
    hr = half * GR
    bar = pltpu.get_barrier_semaphore()
    for dev in (core, across, diag):
        pl.semaphore_signal(bar, inc=1, device_id={"sp": dev}, device_id_type=MESH)
    pl.semaphore_signal(bar, inc=1, device_id={"tp": 1 - tp}, device_id_type=MESH)
    wcopies = [pltpu.make_async_copy(w_ref.at[pl.ds(i * OK, OK), pl.ds(pl.multiple_of(sp * OC, HD), OC)],
                                     wbuf.at[pl.ds(i * OK, OK)], wsem.at[i]) for i in range(HL * HD // OK)]
    for c in wcopies:
        c.start()
    mlbuf[0] = ml_ref[...]

    mine = pl.ds(pl.multiple_of(c01 * hr, GR), hr)
    theirs = pl.ds(pl.multiple_of((1 - c01) * hr, GR), hr)
    mlc = [remote(mlbuf.at[0], mlbuf.at[i + 1], mlsend.at[i], mlrecv.at[i], {"sp": dev})
           for i, dev in enumerate((core, across, diag))]
    c1 = [remote(acc_ref.at[i, theirs], r1.at[i], ssem.at[0, i], rsem.at[0, i], {"sp": core}) for i in range(NG)]
    c2 = [remote(pair.at[i], r2.at[i], ssem.at[1, i], rsem.at[1, i], {"sp": across}) for i in range(NG)]
    c3 = [remote(oall.at[i, mine], oall.at[i, mine], ssem.at[2, i], rsem.at[2, i], {"sp": core}) for i in range(NG)]

    def piece(i, j):
        ya = yall.at[i]
        ys, yr = ysend.at[i], yrecv.at[i]
        return (remote(ypart.at[i, j], yin.at[i, j], ys.at[0, j], yr.at[0, j], {"tp": 1 - tp}),
                remote(ya.at[sp, j], ya.at[sp, j], ys.at[1, j], yr.at[1, j], {"sp": across}),
                remote(ya.at[sp, j], ya.at[sp, j], ys.at[2, j], yr.at[2, j], {"sp": core}),
                remote(ya.at[across, j], ya.at[across, j], ys.at[3, j], yr.at[3, j], {"sp": core}))

    pieces = [[piece(i, j) for j in range(NOC)] for i in range(NG)]

    def columns(table):
        t = jnp.where(c01 == 0, table[:half], table[half:])
        t = jnp.concatenate([t, jnp.zeros((HD - half, HD), jnp.float32)], axis=0)
        return jnp.transpose(t)

    def rows_of(h):
        return pl.ds(pl.multiple_of((c01 * half + h) * GR, GR), GR)

    pl.semaphore_wait(bar, 4)
    mlc[0].start()
    for c in c1:
        c.start()
    mlc[1].start()
    mlc[2].start()

    mlc[0].wait_recv()
    m_pair = jnp.maximum(mlbuf[0], mlbuf[1])
    f_own, f_other = columns(jnp.exp(mlbuf[0] - m_pair)), columns(jnp.exp(mlbuf[1] - m_pair))
    for i in range(NG):
        c1[i].wait_recv()
        seqs = slice(i * GR, (i + 1) * GR)
        for h in range(half):
            rows = slice(h * GR, (h + 1) * GR)
            pair[i, rows, :] = acc_ref[i, rows_of(h), :] * f_own[seqs, h:h + 1] + r1[i, rows, :] * f_other[seqs, h:h + 1]
        c2[i].start()

    mlc[1].wait_recv()
    mlc[2].wait_recv()
    tabs = [mlbuf[i] for i in range(4)]
    m_far = jnp.maximum(tabs[2], tabs[3])
    m_all = jnp.maximum(m_pair, m_far)
    total = jnp.zeros((HL, HD), jnp.float32)
    for t in tabs:
        total = total + jnp.exp(t - m_all) * pltpu.roll(t, HD - B, 1)
    total = jnp.where(lax.broadcasted_iota(jnp.int32, (HL, HD), 1) < B, total, 1.0)
    g_pair, g_far = columns(jnp.exp(m_pair - m_all) / total), columns(jnp.exp(m_far - m_all) / total)
    for c in wcopies:
        c.wait()

    def merge(i):
        c2[i].wait_recv()
        seqs = slice(i * GR, (i + 1) * GR)
        for h in range(half):
            rows = slice(h * GR, (h + 1) * GR)
            oall[i, rows_of(h), :] = pair[i, rows, :] * g_pair[seqs, h:h + 1] + r2[i, rows, :] * g_far[seqs, h:h + 1]
        c3[i].start()

    def project(i, side, j):
        y = jnp.zeros((GR, OCH), jnp.float32)
        for h in range(0, half, 2):
            at = [pl.ds(pl.multiple_of((side * half + h + k) * GR, GR), GR) for k in range(2)]
            lhs = jnp.concatenate([oall[i, at[0], :], oall[i, at[1], :]], axis=1).astype(jnp.bfloat16)
            rhs = wbuf[pl.ds(pl.multiple_of((side * half + h) * HD, HD), 2 * HD), j * OCH:(j + 1) * OCH]
            y = y + jnp.dot(lhs, rhs, preferred_element_type=jnp.float32)
        return y

    def own_heads(i):
        for j in range(NOC):
            ypart[i, j] = project(i, c01, j)

    def other_heads(i):
        c3[i].wait_recv()
        for j in range(NOC):
            ypart[i, j] += project(i, 1 - c01, j)
            pieces[i][j][0].start()

    merge(0)
    own_heads(0)
    for i in range(1, NG):
        merge(i)
        other_heads(i - 1)
        own_heads(i)
    other_heads(NG - 1)
    for i in range(NG):
        for j in range(NOC):
            pieces[i][j][0].wait_recv()
            yall[i, sp, j] = ypart[i, j] + yin[i, j]
            pieces[i][j][1].start()
            pieces[i][j][2].start()
    for i in range(NG):
        for j in range(NOC):
            pieces[i][j][1].wait_recv()
            pieces[i][j][3].start()
    for i in range(NG):
        for j in range(NOC):
            pieces[i][j][2].wait_recv()
            pieces[i][j][3].wait_recv()
        for s in range(4):
            for j in range(NOC):
                seqs = slice(i * GR, (i + 1) * GR)
                at = slice(s * OC + j * OCH, s * OC + (j + 1) * OCH)
                out_ref[seqs, at] = (h_ref[seqs, at].astype(jnp.float32) + yall[i, s, j]).astype(jnp.bfloat16)
    for c in (*c1, *c2, *c3, *mlc, *(c for group in pieces for copies in group for c in copies)):
        c.wait_send()


def solution(mesh):
    half_dim = HD // 2
    freq = 1.0 / (ROPE_BASE ** (np.arange(half_dim, dtype=np.float64) * 2.0 / HD))
    freq = np.concatenate([freq, freq]).astype(np.float32)[None, :]
    f32, bf16 = jnp.float32, jnp.bfloat16
    dma = pltpu.SemaphoreType.DMA

    def shape(dims, dtype):
        return jax.ShapeDtypeStruct(dims, dtype)

    def local_step(hidden, norm_gain, w_query, w_key, w_value, w_out, k_cache, v_cache, positions):
        kt = jnp.transpose(k_cache, (0, 2, 1, 3))
        vt = jnp.transpose(v_cache, (0, 2, 1, 3))
        ring = pltpu.VMEM((SLOTS, HL, SL, HD), bf16)
        g, kring, vring = pl.pallas_call(
            qkv_kernel,
            out_shape=(shape((3, HL * B, HD), f32), ring, ring),
            in_specs=[HBM] * 9,
            out_specs=(VMEM, VMEM, VMEM),
            scratch_shapes=[pltpu.VMEM((3, D, CW), bf16), pltpu.VMEM((B, D), bf16), pltpu.VMEM((3, HL * B, HD), f32),
                            pltpu.SMEM((B,), jnp.int32), pltpu.VMEM((B, D), bf16), pltpu.VMEM((1, D), f32),
                            pltpu.VMEM((1, HD), f32), dma((4,)), dma((3, NKC)), dma((3, 3)), dma((3, 3)), dma((2, EARLY))],
            compiler_params=pltpu.CompilerParams(collective_id=0, has_side_effects=True, vmem_limit_bytes=26 << 20),
            name="qkv",
        )(*(pltpu.with_memory_space_constraint(x, pltpu.HBM) for x in (
            positions, hidden, norm_gain[None, :], jnp.asarray(freq), w_query, w_key, w_value, kt, vt)))

        ko, vo, acc, ml, _, _ = pl.pallas_call(
            cache_kernel,
            out_shape=(shape(kt.shape, bf16), shape(vt.shape, bf16), shape((NG, HL * GR, HD), f32), shape((HL, HD), f32), ring, ring),
            in_specs=[SMEM, VMEM, HBM, HBM, VMEM, VMEM],
            out_specs=(HBM, HBM, VMEM, VMEM, VMEM, VMEM),
            scratch_shapes=[pltpu.VMEM((2, HL, SL), f32), dma((2, SLOTS)), dma((2, SLOTS))],
            input_output_aliases={4: 4, 5: 5},
            compiler_params=pltpu.CompilerParams(vmem_limit_bytes=8 << 20),
            name="cache",
        )(positions, g, kt, vt, kring, vring)

        hr = HL // 2 * GR
        out = pl.pallas_call(
            out_kernel,
            out_shape=shape((B, D), bf16),
            in_specs=[VMEM, VMEM, VMEM, HBM],
            out_specs=VMEM,
            scratch_shapes=[pltpu.VMEM((HL * HD, OC), bf16), pltpu.VMEM((4, HL, HD), f32),
                            pltpu.VMEM((NG, hr, HD), f32), pltpu.VMEM((NG, hr, HD), f32), pltpu.VMEM((NG, hr, HD), f32),
                            pltpu.VMEM((NG, 2 * hr, HD), f32), pltpu.VMEM((NG, NOC, GR, OCH), f32),
                            pltpu.VMEM((NG, NOC, GR, OCH), f32), pltpu.VMEM((NG, 4, NOC, GR, OCH), f32),
                            dma((HL * HD // OK,)), dma((3,)), dma((3,)), dma((3, NG)), dma((3, NG)),
                            dma((NG, 4, NOC)), dma((NG, 4, NOC))],
            compiler_params=pltpu.CompilerParams(collective_id=1, has_side_effects=True, vmem_limit_bytes=18 << 20),
            name="out",
        )(acc, ml, hidden, pltpu.with_memory_space_constraint(w_out, pltpu.HBM))
        return out, jnp.transpose(ko, (0, 2, 1, 3)), jnp.transpose(vo, (0, 2, 1, 3))

    cache_spec = P("dp", "sp", "tp", None)
    specs_in = (P("dp", None), P(None), P(None, "tp"), P(None, "tp"), P(None, "tp"), P("tp", None), cache_spec, cache_spec, P("dp"))
    specs_out = (P("dp", None), cache_spec, cache_spec)
    return jax.shard_map(local_step, mesh=mesh, in_specs=specs_in, out_specs=specs_out, check_vma=False)
```

time: 94.1 us -> 88.3 us (0.938)
  Pallas kernels: 92.6 us -> 86.8 us
    pallas_call x2 -> x1, Pallas kernels: 35.7 us -> 19.4 us  [local_step(): pl.pallas_call(out_kernel, out_shape=shape((B, D), bf16), in_specs=[VMEM,...]
    pallas_call x1, Pallas kernels: 35.9 us -> 50 us  [local_step(): pl.pallas_call(cache_kernel, out_shape=(shape(kt.shape, bf16), shape(vt.s...]
    pallas_call x1, Pallas kernels: 20.9 us -> 17.4 us  [local_step(): pl.pallas_call(qkv_kernel, out_shape=(shape((3, HL * B, HD), f32), ring,...]
where the time goes in v3:
time: 88.3 us; the launch traced here: 88.2 us
  Pallas kernels  86.8 us (98%)
    pallas_call x1, Pallas kernels, local_step(): pl.pallas_call(cache_kernel, out_shape=(shape(kt.shape, bf16), shape(vt.s...  50 us
    pallas_call x1, Pallas kernels, local_step(): pl.pallas_call(out_kernel, out_shape=shape((B, D), bf16), in_specs=[VMEM,...  19.4 us
    pallas_call x1, Pallas kernels, local_step(): pl.pallas_call(qkv_kernel, out_shape=(shape((3, HL * B, HD), f32), ring,...  17.4 us

profile of v3, /device:TPU:0, one launch (start us, length us, event | category | flops | bytes accessed | tf_op | source)
XLA Modules:
  0.0 88.2 jit_solution(343399358820484651)
XLA Ops:
  0.6 0.0 copy-start.1
  0.6 17.4 %qkv.1 = (f32[3,640,128]{2,1,0:T(8,128)S(1)}, bf16[9,20,256,128]{3,2,1,0:T(8,128)(2,1)S(1)}, bf16[9,20,256,128]{3,2,1,0:T(8,128)(2,1)S(1)}) custom-call(s32[32]{0:T(128)} %pos_ref.1, bf16[32,5120]{1,0:T(8,128)(2,1)} %h_ref.1, f32[1,5120]{1,0:T(1,128)} %bitcast.9, f32[1,128]{1,0:T(1,128)} %constant.2.clone.freq_hbm, bf16[5120,2560]{1,0:T(8,128)(2,1)} %wq_ref.1, ...), custom_call_target="tpu_custom_call" | custom-call | tf_op jit(solution)/shard_map/qkv/pallas_call | solution.py:389
  18.1 0.0 copy-done.1
  18.1 0.0 copy-start
  18.1 50.0 %cache.1 = (bf16[32,20,256,128]{3,2,1,0:T(8,128)(2,1)}, bf16[32,20,256,128]{3,2,1,0:T(8,128)(2,1)}, f32[2,320,128]{2,1,0:T(8,128)S(1)}, f32[20,128]{1,0:T(8,128)...) custom-call(s32[32]{0:T(128)S(1)} %copy-done.1, ...), custom_call_target="tpu_custom_call", output_to_operand_aliasing={{4}: (4, {}), {5}: (5, {})} | custom-call | tf_op jit(solution)/shard_map/cache/pallas_call | solution.py:402
  68.1 0.0 copy-done
  68.1 19.4 %out.1 = bf16[32,5120]{1,0:T(8,128)(2,1)S(1)} custom-call(f32[2,320,128]{2,1,0:T(8,128)S(1)} %get-tuple-element.13.acc_ref, f32[20,128]{1,0:T(8,128)S(1)} %get-tuple-element.14.ml_ref, bf16[32,5120]{1,0:T(8,128)(2,1)S(1)} %copy-done, bf16[2560,5120]{1,0:T(8,128)(2,1)} %w_ref.1), custom_call_target="tpu_custom_call" | custom-call | tf_op jit(solution)/shard_map/out/pallas_call | solution.py:414
  87.5 0.7 copy.18
Async XLA Ops:
  0.6 17.4 %copy-start.1 = (s32[32]{0:T(128)S(1)}, s32[32]{0:T(128)}, u32[]{:S(2)}) copy-start(s32[32]{0:T(128)} %pos_ref.1) | copy-start | bytes 388
  18.1 50.0 %copy-start = (bf16[32,5120]{1,0:T(8,128)(2,1)S(1)}, bf16[32,5120]{1,0:T(8,128)(2,1)}, u32[]{:S(2)}) copy-start(bf16[32,5120]{1,0:T(8,128)(2,1)} %h_ref.1) | copy-start | bytes 983044

commit v4 on v3

--- a/solution.py
+++ b/solution.py
@@ -23,14 +23,16 @@
 KC = 1280
 NKC = D // KC
 OC = 1280
-OCH = 256
+OCH = 640
 NOC = OC // OCH
 OK = 512
 GR = 16
 NG = B // GR
-SLOTS = 9
+SLOTS = 8
 EARLY = 8
-AHEAD = 5
+BURST = 4
+LEAD = 3
+JOBS = ((0, 0, 5), (1, 0, 5), (2, 0, 5))
 WINDOW = 5
 SCALE = HD ** -0.5
 HBM = pl.BlockSpec(memory_space=pltpu.HBM)
@@ -54,18 +56,19 @@
     bar = pltpu.get_barrier_semaphore()
     for dev in (across, core):
         pl.semaphore_signal(bar, inc=1, device_id={"sp": dev}, device_id_type=MESH)
-    cols = pl.ds(pl.multiple_of(sp * CW, HD), CW)
     small = [pltpu.make_async_copy(src, dst, insem.at[i]) for i, (src, dst) in enumerate(
         ((h_hbm, h_ref), (gain_hbm, gain_ref), (freq_hbm, freq_ref), (pos_hbm, pos_ref)))]
     for c in small:
         c.start()
 
-    def chunk(kind, c):
+    def chunk(job, c):
+        kind, first, heads = JOBS[job]
         src = (wq_ref, wk_ref, wv_ref)[kind]
         rows = pl.ds(c * KC, KC)
-        return pltpu.make_async_copy(src.at[rows, cols], wbuf.at[kind, rows], wsem.at[kind, c])
-
-    chunks = [chunk(kind, c) for kind in range(3) for c in range(NKC)]
+        cols = pl.ds(pl.multiple_of(sp * CW + first * HD, HD), heads * HD)
+        return pltpu.make_async_copy(src.at[rows, cols], wbuf.at[kind, rows, first * HD:(first + heads) * HD], wsem.at[job, c])
+
+    chunks = [chunk(job, c) for job in range(len(JOBS)) for c in range(NKC)]
     tiles = [pltpu.make_async_copy(src.at[b], dst.at[b], tsem.at[i, b])
              for b in range(EARLY) for i, (src, dst) in enumerate(((k_ref, kring), (v_ref, vring)))]
     queue = chunks + tiles
@@ -88,39 +91,41 @@
     sine = jnp.where(lane < HD // 2, -sine, sine)
     pl.semaphore_wait(bar, 2)
 
-    own = pl.ds(pl.multiple_of(sp * HS * B, B), HS * B)
-    far = pl.ds(pl.multiple_of(across * HS * B, B), HS * B)
-    links = [(remote(g.at[kind, own], g.at[kind, own], ssem.at[kind, 0], rsem.at[kind, 0], {"sp": across}),
-              remote(g.at[kind, own], g.at[kind, own], ssem.at[kind, 1], rsem.at[kind, 1], {"sp": core}),
-              remote(g.at[kind, far], g.at[kind, far], ssem.at[kind, 2], rsem.at[kind, 2], {"sp": core}))
-             for kind in range(3)]
-
-    for kind in range(3):
-        acc = jnp.zeros((B, CW), jnp.float32)
+    def link(job):
+        kind, first, heads = JOBS[job]
+        own, far = (g.at[kind, pl.ds(pl.multiple_of(dev * HS * B + first * B, B), heads * B)] for dev in (sp, across))
+        return [remote(ref, ref, ssem.at[job, i], rsem.at[job, i], {"sp": dev})
+                for i, (ref, dev) in enumerate(((own, across), (own, core), (far, core)))]
+
+    links = [link(job) for job in range(len(JOBS))]
+    for job, (kind, first, heads) in enumerate(JOBS):
+        acc = jnp.zeros((B, heads * HD), jnp.float32)
         for c in range(NKC):
-            step = kind * NKC + c
+            step = job * NKC + c
             chunks[step].wait()
             queue[step + WINDOW].start()
             rows = slice(c * KC, (c + 1) * KC)
-            acc = acc + jnp.dot(xn[:, rows], wbuf[kind, rows, :], preferred_element_type=jnp.float32)
-        for i in range(HS):
+            acc = acc + jnp.dot(xn[:, rows], wbuf[kind, rows, first * HD:(first + heads) * HD],
+                                preferred_element_type=jnp.float32)
+        for i in range(heads):
             u = acc[:, i * HD:(i + 1) * HD]
             if kind < 2:
                 u = u * cosine + pltpu.roll(u, HD // 2, 1) * sine
-            g[kind, pl.ds(pl.multiple_of(sp * HS * B + i * B, B), B), :] = u.astype(jnp.bfloat16).astype(jnp.float32)
-        links[kind][0].start()
-        links[kind][1].start()
-        if kind > 0:
-            links[kind - 1][0].wait_recv()
-            links[kind - 1][2].start()
+            at = pl.ds(pl.multiple_of(sp * HS * B + (first + i) * B, B), B)
+            g[kind, at, :] = u.astype(jnp.bfloat16).astype(jnp.float32)
+        links[job][0].start()
+        links[job][1].start()
+        if job > 0:
+            links[job - 1][0].wait_recv()
+            links[job - 1][2].start()
     for c in queue[len(chunks) + WINDOW:]:
         c.start()
-    links[2][0].wait_recv()
-    links[2][2].start()
-    for kind in range(3):
-        links[kind][0].wait_send()
-        links[kind][1].wait()
-        links[kind][2].wait()
+    links[-1][0].wait_recv()
+    links[-1][2].start()
+    for link in links:
+        link[0].wait_send()
+        link[1].wait()
+        link[2].wait()
     out_ref[...] = g[...]
     for c in tiles:
         c.wait()
@@ -181,16 +186,9 @@
         slot = lax.rem(b, SLOTS)
         return pltpu.make_async_copy(vbuf.at[slot], vo_ref.at[b], wsem.at[1, slot])
 
-    for b in range(EARLY, SLOTS):
-        for c in reads(b):
-            c.start()
     ml_ref[...] = jnp.zeros_like(ml_ref)
 
     def arrive(b):
-        @pl.when(b >= EARLY)
-        def _():
-            for c in reads(b):
-                c.wait()
         slot = lax.rem(b, SLOTS)
         insert_row(g_ref, b, pos_ref[b] - base, ((1, kbuf, slot), (2, vbuf, slot)))
 
@@ -210,33 +208,57 @@
         acc_ref[b // GR, pl.ds(lax.rem(b, GR), HL, stride=GR), :] = weighted(p, lambda h: vbuf[slot, h])
         put_stats(ml_ref, b, m, total)
 
-    def ahead(b):
-        @pl.when((b + AHEAD >= SLOTS) & (b + AHEAD < B))
-        def _():
-            write_k(b + AHEAD - SLOTS).wait()
-            write_v(b + AHEAD - SLOTS).wait()
-            for c in reads(b + AHEAD):
-                c.start()
-
-    arrive(0)
-    ahead(0)
-    score(0)
-    write_k(0).start()
-    write_v(0).start()
-
-    @pl.loop(1, B)
-    def _(b):
-        arrive(b)
-        ahead(b)
-        score(b)
-        value(b - 1)
+    def write(b):
         write_k(b).start()
         write_v(b).start()
 
-    value(B - 1)
-    for b in range(B - SLOTS, B):
+    def landed(b):
+        for c in reads(b):
+            c.wait()
+
+    for b in range(BURST):
+        arrive(b)
+    for b in range(BURST):
+        write(b)
+
+    groups = B // BURST
+
+    def refill(b, more):
         write_k(b).wait()
         write_v(b).wait()
+
+        @pl.when(more)
+        def _():
+            for c in reads(b + SLOTS):
+                c.start()
+
+    @pl.loop(0, groups)
+    def _(i):
+        first = i * BURST
+        more = i + 2 < groups
+        score(first)
+        for b in range(1, BURST):
+            score(first + b)
+            value(first + b - 1)
+            refill(first + b - 1, more)
+        value(first + BURST - 1)
+        refill(first + BURST - 1, more)
+
+        @pl.when(i + 1 < groups)
+        def _():
+            @pl.when(i > 0)
+            def _():
+                for t in range(BURST - LEAD, BURST):
+                    landed(first + BURST + t)
+            for t in range(BURST):
+                arrive(first + BURST + t)
+
+            @pl.when(more)
+            def _():
+                for t in range(BURST - LEAD):
+                    landed(first + 2 * BURST + t)
+            for t in range(BURST):
+                write(first + BURST + t)
 
 
 def out_kernel(acc_ref, ml_ref, h_ref, w_ref, out_ref,
@@ -393,7 +415,7 @@
             out_specs=(VMEM, VMEM, VMEM),
             scratch_shapes=[pltpu.VMEM((3, D, CW), bf16), pltpu.VMEM((B, D), bf16), pltpu.VMEM((3, HL * B, HD), f32),
                             pltpu.SMEM((B,), jnp.int32), pltpu.VMEM((B, D), bf16), pltpu.VMEM((1, D), f32),
-                            pltpu.VMEM((1, HD), f32), dma((4,)), dma((3, NKC)), dma((3, 3)), dma((3, 3)), dma((2, EARLY))],
+                            pltpu.VMEM((1, HD), f32), dma((4,)), dma((len(JOBS), NKC)), dma((len(JOBS), 3)), dma((len(JOBS), 3)), dma((2, EARLY))],
             compiler_params=pltpu.CompilerParams(collective_id=0, has_side_effects=True, vmem_limit_bytes=26 << 20),
             name="qkv",
         )(*(pltpu.with_memory_space_constraint(x, pltpu.HBM) for x in (

time: 88.3 us -> 87 us (0.985)
  Pallas kernels: 86.8 us -> 85.4 us
where the time goes in v4:
time: 87 us; the launch traced here: 86.8 us
  Pallas kernels  85.4 us (98%)
    pallas_call x1, Pallas kernels, local_step(): pl.pallas_call(cache_kernel, out_shape=(shape(kt.shape, bf16), shape(vt.s...  49.3 us
    pallas_call x1, Pallas kernels, local_step(): pl.pallas_call(out_kernel, out_shape=shape((B, D), bf16), in_specs=[VMEM,...  18.6 us
    pallas_call x1, Pallas kernels, local_step(): pl.pallas_call(qkv_kernel, out_shape=(shape((3, HL * B, HD), f32), ring,...  17.4 us

profile of v4, /device:TPU:0, one launch (start us, length us, event | category | flops | bytes accessed | tf_op | source)
XLA Modules:
  0.0 86.8 jit_solution(17626312986377415519)
XLA Ops:
  0.6 0.0 copy-start.1
  0.6 17.4 %qkv.1 = (f32[3,640,128]{2,1,0:T(8,128)S(1)}, bf16[8,20,256,128]{3,2,1,0:T(8,128)(2,1)S(1)}, bf16[8,20,256,128]{3,2,1,0:T(8,128)(2,1)S(1)}) custom-call(s32[32]{0:T(128)} %pos_ref.1, bf16[32,5120]{1,0:T(8,128)(2,1)} %h_ref.1, f32[1,5120]{1,0:T(1,128)} %bitcast.9, f32[1,128]{1,0:T(1,128)} %constant.2.clone.freq_hbm, bf16[5120,2560]{1,0:T(8,128)(2,1)} %wq_ref.1, ...), custom_call_target="tpu_custom_call" | custom-call | tf_op jit(solution)/shard_map/qkv/pallas_call | solution.py:411
  18.1 0.0 copy-done.1
  18.1 0.0 copy-start
  18.1 49.3 %cache.1 = (bf16[32,20,256,128]{3,2,1,0:T(8,128)(2,1)}, bf16[32,20,256,128]{3,2,1,0:T(8,128)(2,1)}, f32[2,320,128]{2,1,0:T(8,128)S(1)}, f32[20,128]{1,0:T(8,128)...) custom-call(s32[32]{0:T(128)S(1)} %copy-done.1, ...), custom_call_target="tpu_custom_call", output_to_operand_aliasing={{4}: (4, {}), {5}: (5, {})} | custom-call | tf_op jit(solution)/shard_map/cache/pallas_call | solution.py:424
  67.4 0.0 copy-done
  67.4 18.6 %out.1 = bf16[32,5120]{1,0:T(8,128)(2,1)S(1)} custom-call(f32[2,320,128]{2,1,0:T(8,128)S(1)} %get-tuple-element.13.acc_ref, f32[20,128]{1,0:T(8,128)S(1)} %get-tuple-element.14.ml_ref, bf16[32,5120]{1,0:T(8,128)(2,1)S(1)} %copy-done, bf16[2560,5120]{1,0:T(8,128)(2,1)} %w_ref.1), custom_call_target="tpu_custom_call" | custom-call | tf_op jit(solution)/shard_map/out/pallas_call | solution.py:436
  86.1 0.7 copy.18
Async XLA Ops:
  0.6 17.4 %copy-start.1 = (s32[32]{0:T(128)S(1)}, s32[32]{0:T(128)}, u32[]{:S(2)}) copy-start(s32[32]{0:T(128)} %pos_ref.1) | copy-start | bytes 388
  18.1 49.4 %copy-start = (bf16[32,5120]{1,0:T(8,128)(2,1)S(1)}, bf16[32,5120]{1,0:T(8,128)(2,1)}, u32[]{:S(2)}) copy-start(bf16[32,5120]{1,0:T(8,128)(2,1)} %h_ref.1) | copy-start | bytes 983044
